TPU v7x, 32 devices: a 4x2x2 block of a 4x4x8 slice. The times are simulated.
32 devices in a mesh: dp: 4 (over y, z), tp: 8 (over x, core).
Axes of the slice: x: 4, y: 2, z: 2, core: 2. Of those that a mesh axis runs over, the one named last changes fastest.
The devices are a block of a 4x4x8 slice.
Arguments:
- x: bfloat16 [32, 256, 6144], P('dp'), parts along dimension 0
- seq_lens: int32 [32], P('dp'), parts along dimension 0
- w_query: bfloat16 [6144, 6144], P(None, 'tp')
- w_key: bfloat16 [6144, 1024], P(None, 'tp')
- w_value: bfloat16 [6144, 1024], P(None, 'tp')
- w_out: bfloat16 [6144, 6144], P('tp')
- w_gate: bfloat16 [6144, 16384], P(None, 'tp')
- w_up: bfloat16 [6144, 16384], P(None, 'tp')
- w_down: bfloat16 [16384, 6144], P('tp')
- attn_gain: bfloat16 [6144], replicated
- mlp_gain: bfloat16 [6144], replicated
- k_cache: bfloat16 [32, 512, 8, 128], P('dp', None, 'tp'), parts along dimension 0
- v_cache: bfloat16 [32, 512, 8, 128], P('dp', None, 'tp'), parts along dimension 0
Outputs:
- output 1: bfloat16 [32, 256, 6144], P('dp'), parts along dimension 0
- output 2: bfloat16 [32, 512, 8, 128], P('dp', None, 'tp'), parts along dimension 0
- output 3: bfloat16 [32, 512, 8, 128], P('dp', None, 'tp'), parts along dimension 0
There are 4 independent parts. A program takes and returns all parts, laid end to end along the dimension named above; an argument that names none is the same for every part.
All inputs are finite; a program needn't handle non-finite values.
Results may differ from a plain program's by a relative error of at most 0.0113029.
Values are sent between devices in bfloat16 or wider.
A program may use at most 768 MiB of HBM per device.

v0:
```python
import jax
import jax.numpy as jnp
from jax import lax
from jax.sharding import PartitionSpec as P

EPS = 1e-5
ROPE_BASE = 10000.0


def rms_norm(rows, gain):
    rows32 = rows.astype(jnp.float32)
    inv_rms = lax.rsqrt(jnp.mean(rows32 * rows32, axis=-1, keepdims=True) + EPS)
    return (rows32 * inv_rms * gain.astype(jnp.float32)).astype(jnp.bfloat16)


def rotary(vecs):
    seq_len = vecs.shape[1]
    head_dim = vecs.shape[-1]
    half_dim = head_dim // 2
    inv_freq = ROPE_BASE ** (-jnp.arange(0, head_dim, 2).astype(jnp.float32) / head_dim)
    angles = jnp.arange(seq_len).astype(jnp.float32)[:, None] * inv_freq[None, :]
    table_shape = (1, seq_len) + (1,) * (vecs.ndim - 3) + (half_dim,)
    cos_tab = jnp.cos(angles).reshape(table_shape)
    sin_tab = jnp.sin(angles).reshape(table_shape)
    pairs = vecs.reshape(vecs.shape[:-1] + (half_dim, 2))
    even_part = pairs[..., 0]
    odd_part = pairs[..., 1]
    turned = jnp.stack([even_part * cos_tab - odd_part * sin_tab, even_part * sin_tab + odd_part * cos_tab], axis=-1)
    return turned.reshape(vecs.shape).astype(jnp.bfloat16)


def causal_attention(queries, keys, values, seq_lens):
    seq_len = queries.shape[1]
    head_dim = queries.shape[-1]
    scores = jnp.einsum("bqkgh,bskh->bkgqs", queries, keys, preferred_element_type=jnp.float32) * head_dim ** -0.5
    positions = jnp.arange(seq_len)
    allowed = (positions[None, None, :] <= positions[None, :, None]) & (positions[None, None, :] < seq_lens[:, None, None])
    scores = jnp.where(allowed[:, None, None], scores, -jnp.inf)
    probs = jax.nn.softmax(scores, axis=-1).astype(jnp.bfloat16)
    return jnp.einsum("bkgqs,bskh->bqkgh", probs, values, preferred_element_type=jnp.float32).astype(jnp.bfloat16)


def sum_partials(partial, resid_rows, tp_size):
    batch_size, seq_len, model_width = partial.shape
    stacked = partial.reshape(batch_size, tp_size, seq_len // tp_size, model_width)
    received = lax.all_to_all(stacked, "tp", 1, 1, tiled=True)
    summed = jnp.sum(received.astype(jnp.float32), axis=1)
    return (resid_rows.astype(jnp.float32) + summed).astype(jnp.bfloat16)


def solution(mesh):
    tp_size = mesh.shape["tp"]

    def layer_shard(x, seq_lens, w_query, w_key, w_value, w_out, w_gate, w_up, w_down, attn_gain, mlp_gain, k_cache, v_cache):
        batch_size, seq_len, model_width = x.shape
        head_dim = k_cache.shape[3]
        kv_local = k_cache.shape[2]
        group_size = w_query.shape[1] // (head_dim * kv_local)
        rows_each = seq_len // tp_size
        tp_index = lax.axis_index("tp")
        normed = rms_norm(x, attn_gain)
        queries = rotary(jnp.einsum("bsd,dk->bsk", normed, w_query, preferred_element_type=jnp.float32).reshape(batch_size, seq_len, kv_local, group_size, head_dim))
        keys = rotary(jnp.einsum("bsd,dk->bsk", normed, w_key, preferred_element_type=jnp.float32).reshape(batch_size, seq_len, kv_local, head_dim))
        values = jnp.einsum("bsd,dk->bsk", normed, w_value, preferred_element_type=jnp.float32).astype(jnp.bfloat16).reshape(batch_size, seq_len, kv_local, head_dim)
        valid = (jnp.arange(seq_len)[None, :] < seq_lens[:, None])[:, :, None, None]
        keys = jnp.where(valid, keys, jnp.zeros_like(keys))
        values = jnp.where(valid, values, jnp.zeros_like(values))
        k_cache_out = lax.dynamic_update_slice(k_cache, keys, (0, 0, 0, 0))
        v_cache_out = lax.dynamic_update_slice(v_cache, values, (0, 0, 0, 0))
        attn_rows = causal_attention(queries, keys, values, seq_lens).reshape(batch_size, seq_len, -1)
        attn_part = jnp.einsum("bsk,kd->bsd", attn_rows, w_out, preferred_element_type=jnp.float32).astype(jnp.bfloat16)
        x_rows = lax.dynamic_slice_in_dim(x, tp_index * rows_each, rows_each, axis=1)
        hidden_rows = sum_partials(attn_part, x_rows, tp_size)
        normed_mlp = lax.all_gather(rms_norm(hidden_rows, mlp_gain), "tp", axis=1, tiled=True)
        gate_pre = jnp.einsum("bsd,df->bsf", normed_mlp, w_gate, preferred_element_type=jnp.float32)
        up_pre = jnp.einsum("bsd,df->bsf", normed_mlp, w_up, preferred_element_type=jnp.float32)
        gated = (jax.nn.silu(gate_pre) * up_pre).astype(jnp.bfloat16)
        mlp_part = jnp.einsum("bsf,fd->bsd", gated, w_down, preferred_element_type=jnp.float32).astype(jnp.bfloat16)
        out_rows = sum_partials(mlp_part, hidden_rows, tp_size)
        y = lax.all_gather(out_rows, "tp", axis=1, tiled=True)
        return y, k_cache_out, v_cache_out

    cache_spec = P("dp", None, "tp", None)
    return jax.shard_map(layer_shard, mesh=mesh, in_specs=(P("dp", None, None), P("dp"), P(None, "tp"), P(None, "tp"), P(None, "tp"), P("tp", None), P(None, "tp"), P(None, "tp"), P("tp", None), P(), P(), cache_spec, cache_spec), out_specs=(P("dp", None, None), cache_spec, cache_spec), check_vma=False)
```

profile of v0, /device:TPU:81, one launch (start us, length us, event | category | flops | bytes accessed | tf_op | source)
XLA Modules:
  0.0 1222.3 jit_solution(4938966492286812969)
XLA Ops:
  7.2 0.0 copy-start
  7.2 2.4 copy.67
  9.6 0.7 convert_element_type.129
  10.3 10.3 fusion
  20.7 13.1 %fusion.14 = f32[8,256,128]{1,2,0:T(8,128)S(1)} fusion(bf16[8,256,6144]{2,1,0:T(8,128)(2,1)} %param.13, f32[6144]{0:T(1024)S(1)} %convert_element_type.129, f32[8,256]{1,0:T(8,128)S(1)} %add_rsqrt_fusion, bf16[6144,128]{1,0:T(8,128)(2,1)} %param.16), kind=kOutput, calls=%fused_computation.17 | convolution fusion | flops 3271557120 | bytes 27820032 | tf_op jit(solution)/shard_map/bsd,dk->bsk/dot_general | solution.py:63
  33.8 0.6 copy.56
  34.4 0.3 multiply_cosine_fusion
  34.7 0.1 multiply_subtract_fusion
  34.9 0.0 copy-start.3
  35.0 1.2 copy.38
  36.1 27.0 %fusion.12 = f32[8,256,768]{2,1,0:T(8,128)} fusion(bf16[8,256,6144]{2,1,0:T(8,128)(2,1)} %param.13, f32[6144]{0:T(1024)S(1)} %convert_element_type.129, f32[8,256]{1,0:T(8,128)S(1)} %add_rsqrt_fusion, bf16[6144,768]{1,0:T(8,128)(2,1)} %param.15), kind=kOutput, calls=%fused_computation.16 | convolution fusion | flops 19377684480 | bytes 40927232 | tf_op jit(solution)/shard_map/bsd,dk->bsk/dot_general | solution.py:62
  63.2 6.6 copy.39
  69.8 3.8 subtract_convert_fusion
  73.6 0.0 copy-done.12
  73.6 0.1 iota_compare_fusion.1
  73.7 0.3 pad_maximum_fusion
  74.0 0.5 broadcast_and_fusion
  74.4 0.0 copy-start.5
  74.4 3.4 fusion.19
  77.8 3.9 fusion.18
  81.7 0.0 copy-done.9
  81.7 0.0 copy-done
  81.7 12.4 %bitcast_dynamic-update-slice_fusion = (bf16[8,512,1,128]{3,1,2,0:T(8,128)(2,1)}, bf16[8,256,128]{2,1,0:T(8,128)(2,1)}) fusion(bf16[8,512,1,128]{3,1,2,0:T(8,128)(2,1)} %copy.67, bf16[6144,128]{1,0:T(8,128)(2,1)S(1)} %copy-done, bf16[8,256,6144]{2,1,0:T(8,128)(2,1)} %param.13, f32[6144]{0:T(1024)S(1)} %convert_element_type.129, ...), kind=kOutput, calls=%fused_computation.51 | convolution fusion | flops 3272081408 | bytes 27822080 | tf_op jit(solution)/shard_map/bsd,dk->bsk/dot_general | solution.py:64
  94.2 6.0 fusion.32
  100.2 26.9 %convolution_convert_fusion = bf16[8,256,6144]{2,1,0:T(8,128)(2,1)} fusion(bf16[8,256,768]{1,2,0:T(8,128)(2,1)} %bitcast.88, bf16[768,6144]{1,0:T(8,128)(2,1)} %param.18), kind=kOutput, calls=%fused_computation.14 | convolution fusion | flops 19339935744 | bytes 37748736 | tf_op jit(solution)/shard_map/bsk,kd->bsd/dot_general | solution.py:71
  127.1 21.0 %copy.44 = bf16[8,8,32,6144]{3,2,0,1:T(8,128)(2,1)} copy(bf16[8,8,32,6144]{3,2,1,0:T(8,128)(2,1)} %bitcast.82) | data formatting | bytes 50331648 | tf_op jit(solution)/shard_map/reshape | solution.py:45
  148.2 8.4 all-to-all-start
  156.6 273.4 %all-to-all-done = bf16[8,8,32,6144]{3,2,0,1:T(8,128)(2,1)} async-done(((bf16[8,8,32,6144]{3,2,0,1:T(8,128)(2,1)}), bf16[8,8,32,6144]{3,2,0,1:T(8,128)(2,1)}, u32[]{:S(2)}, u32[]{:S(2)}) %all-to-all-start) | async-done | bytes 25165856 | tf_op jit(solution)/shard_map/all_to_all | solution.py:46
  430.0 16.5 %convert_reduce_fusion.1 = f32[8,32,6144]{2,1,0:T(8,128)} fusion(bf16[8,8,32,6144]{3,2,0,1:T(8,128)(2,1)} %all-to-all-done), kind=kLoop, calls=%fused_computation.6 | loop fusion | flops 23592960 | bytes 31457280 | tf_op jit(solution)/shard_map/reduce_sum | solution.py:47
  446.4 5.0 fusion.23
  451.4 1.6 copy-done.2
  453.1 2.6 fusion.25
  455.6 0.1 all-gather.3.cloned.1.call-update
  455.7 0.1 all-gather.5.cloned.1.call-start
  455.8 119.2 %all-gather.3.cloned.1.call-done = bf16[8,256,6144]{2,1,0:T(8,128)(2,1)} async-done(((bf16[8,32,6144]{2,1,0:T(8,128)(2,1)}), bf16[8,256,6144]{2,1,0:T(8,128)(2,1)}) %all-gather.3.cloned.1.call-update) | async-done | bytes 25165840 | tf_op jit(solution)/shard_map/all_gather | solution.py:74
  575.0 61.4 %fusion.5 = f32[8,256,2048]{2,1,0:T(8,128)} fusion(bf16[8,256,6144]{2,1,0:T(8,128)(2,1)} %all-gather.3.cloned.1.call-done, bf16[6144,2048]{1,0:T(8,128)(2,1)} %param.20), kind=kOutput, calls=%fused_computation.9 | convolution fusion | flops 51539607552 | bytes 67108864 | tf_op jit(solution)/shard_map/bsd,df->bsf/dot_general | solution.py:76
  636.4 61.4 %fusion.7 = f32[8,256,2048]{2,1,0:T(8,128)} fusion(bf16[8,256,6144]{2,1,0:T(8,128)(2,1)} %all-gather.3.cloned.1.call-done, bf16[6144,2048]{1,0:T(8,128)(2,1)} %param.19), kind=kOutput, calls=%fused_computation.11 | convolution fusion | flops 51539607552 | bytes 67108864 | tf_op jit(solution)/shard_map/bsd,df->bsf/dot_general | solution.py:75
  697.8 65.4 %fusion.9 = bf16[8,256,6144]{2,1,0:T(8,128)(2,1)} fusion(bf16[2048,6144]{1,0:T(8,128)(2,1)} %param.21, f32[8,256,2048]{2,1,0:T(8,128)} %fusion.5, f32[8,256,2048]{2,1,0:T(8,128)} %fusion.7), kind=kOutput, calls=%fused_computation.15 | convolution fusion | flops 51577356288 | bytes 83886080 | tf_op jit(solution)/shard_map/bsf,fd->bsd/dot_general | solution.py:78
  763.3 12.0 copy.45
  775.2 277.8 %all_to_all.10 = bf16[8,8,32,6144]{3,2,0,1:T(8,128)(2,1)} all-to-all(bf16[8,8,32,6144]{3,2,0,1:T(8,128)(2,1)S(1)} %copy.45), channel_id=1, replica_groups=mesh['dp'=4,'tp'=8] {'tp'}, dimensions={1} | all-to-all | bytes 50331648 | tf_op jit(solution)/shard_map/all_to_all | solution.py:46
  1053.0 16.5 %convert_reduce_fusion = f32[8,32,6144]{2,1,0:T(8,128)} fusion(bf16[8,8,32,6144]{3,2,0,1:T(8,128)(2,1)} %all_to_all.10), kind=kLoop, calls=%fused_computation.5 | loop fusion | flops 23592960 | bytes 31457280 | tf_op jit(solution)/shard_map/reduce_sum | solution.py:47
  1069.5 6.4 fusion.26
  1075.8 0.1 all-gather.5.cloned.1.call-update
  1076.0 0.4 copy.46
  1076.4 0.1 constant_dynamic-update-slice_fusion
  1076.5 0.0 copy-start.6
  1076.5 117.4 %all-gather.5.cloned.1.call-done = bf16[8,256,6144]{2,1,0:T(8,128)(2,1)} async-done(((bf16[8,32,6144]{2,1,0:T(8,128)(2,1)}), bf16[8,256,6144]{2,1,0:T(8,128)(2,1)}) %all-gather.5.cloned.1.call-update) | async-done | bytes 25165840 | tf_op jit(solution)/shard_map/all_gather | solution.py:80
  1193.9 21.1 %copy.68 = bf16[8,256,6144]{2,1,0:T(8,128)(2,1)} copy(bf16[8,256,6144]{2,1,0:T(8,128)(2,1)} %all-gather.5.cloned.1.call-done) | data formatting | bytes 50331648
  (27 shorter events, 0.2 us)
Async XLA Ops:
  7.2 74.5 %copy-start = (bf16[6144,128]{1,0:T(8,128)(2,1)S(1)}, bf16[6144,128]{1,0:T(8,128)(2,1)}, u32[]{:S(2)}) copy-start(bf16[6144,128]{1,0:T(8,128)(2,1)} %param.17) | copy-start | bytes 4718596
  34.9 28.2 %copy-start.3 = (bf16[8,256,1,64,2]{1,0,4,3,2:T(8,128)(2,1)}, bf16[8,256,1,64,2]{1,0,4,3,2:T(8,128)(2,1)S(1)}, u32[]{:S(2)}) copy-start(bf16[8,256,1,64,2]{1,0,4,3,2:T(8,128)(2,1)S(1)} %maximum_convert_fusion) | copy-start | bytes 1572868
  63.2 10.4 copy-start.12
  69.8 4.6 copy-start.8
  73.7 8.0 copy-start.9
  74.4 3.4 copy-start.5
  148.2 8.5 copy-start.11
  148.2 281.8 %all-to-all-start = ((bf16[8,8,32,6144]{3,2,0,1:T(8,128)(2,1)}), bf16[8,8,32,6144]{3,2,0,1:T(8,128)(2,1)}, u32[]{:S(2)}, u32[]{:S(2)}) async-start(bf16[8,8,32,6144]{3,2,0,1:T(8,128)(2,1)} %copy.44), calls=%async_computation | async-start | bytes 50331648 | tf_op jit(solution)/shard_map/all_to_all | solution.py:46
  156.6 418.4 %all-gather.3.cloned.1.call-start = ((), (), s32[]{:S(2)}) async-start(), calls=%async_computation.2 | async-start | bytes 28311552 | tf_op jit(solution)/shard_map/all_gather | solution.py:74
  451.4 1.6 copy-start.2
  455.7 738.2 %all-gather.5.cloned.1.call-start = ((), (), s32[]{:S(2)}) async-start(), calls=%async_computation.3 | async-start | bytes 28311552 | tf_op jit(solution)/shard_map/all_gather | solution.py:80
  1069.5 6.4 copy-start.4
  1069.5 6.5 copy-start.10
  1069.5 6.9 copy-start.7
  1076.5 138.6 %copy-start.6 = (bf16[8,512,1,128]{3,1,2,0:T(8,128)(2,1)}, bf16[8,512,1,128]{3,1,2,0:T(8,128)(2,1)S(1)}, u32[]{:S(2)}) copy-start(bf16[8,512,1,128]{3,1,2,0:T(8,128)(2,1)S(1)} %constant_dynamic-update-slice_fusion) | copy-start | bytes 3145732
  1193.9 21.1 %copy-start.1 = (bf16[6144,128]{1,0:T(8,128)(2,1)S(1)}, bf16[6144,128]{1,0:T(8,128)(2,1)}, u32[]{:S(2)}) copy-start(bf16[6144,128]{1,0:T(8,128)(2,1)} %param.17) | copy-start | bytes 4718596
Sparse Core Ops, SparseCore 0:
  455.8 119.1 all-gather.2
  1076.0 117.8 all-gather.4
where the time goes:
time: 1230 us; the launch traced here: 1220 us
  waiting for transfers between devices  510 us (41%)
  blocking collectives  278 us (23%)
  matrix products  277 us (23%)
  local copies, waits for them, and re-layouts  67.2 us (5%)
  other arithmetic  66.9 us (5%)
  between operations  14.7 us (1%)
    all_to_all x1, blocking collectives, sum_partials(): received = lax.all_to_all(stacked, 'tp', 1, 1, tiled=True)  278 us
    all_to_all x1, waiting for transfers between devices, sum_partials(): received = lax.all_to_all(stacked, 'tp', 1, 1, tiled=True)  273 us
    all_gather x1, waiting for transfers between devices, layer_shard(): lax.all_gather(rms_norm(hidden_rows, mlp_gain), 'tp', axis=1, tiled=True)  119 us
    all_gather x1, waiting for transfers between devices, layer_shard(): y = lax.all_gather(out_rows, 'tp', axis=1, tiled=True)  117 us
    dot_general x1, matrix products, layer_shard(): jnp.einsum('bsf,fd->bsd', gated, w_down, preferred_element_type=jnp.float32)  65.4 us
    dot_general x1, matrix products, layer_shard(): jnp.einsum('bsd,df->bsf', normed_mlp, w_gate, preferred_element_type=jnp....  61.4 us
    dot_general x1, matrix products, layer_shard(): jnp.einsum('bsd,df->bsf', normed_mlp, w_up, preferred_element_type=jnp.fl...  61.4 us
    reshape x2, local copies, waits for them, and re-layouts, sum_partials(): partial.reshape(batch_size, tp_size, seq_len // tp_size, model_width)  33 us
  transfers between devices with their start and end apart: 3, of which 3 were waited for; matrix products, arithmetic and copies ran while one was open for 0% of the time, Pallas kernels for 0%

commit v1 on v0

v1 whole, which is shorter than its diff:
```python
import functools

import jax
import jax.numpy as jnp
from jax import lax
from jax.experimental import pallas as pl
from jax.experimental.pallas import tpu as pltpu
from jax.sharding import PartitionSpec as P


EPS = 1e-5
ROPE_BASE = 10000.0
CHUNKS = (1, 2, 2, 2, 1)
CORES = 2
TP_CHIPS = 4

STAGES = (("QKV", 13), ("OUT", 15), ("B", 5), ("C", 1.5), ("D", 3.5), ("E", 1), ("F", .5), ("MLP", 46), ("B", 5), ("C", 1.5), ("D", 3), ("E", 1), ("F", .5), ("Y", 5))
LINK = {"B": 33.7, "C": 16.9, "D": 16.9, "E": 8.4}
DIE = {"OUT": 4.7, "F": 4.7, "MLP": 4.7}
LOOK_AHEAD = 6


def stage_order(chunks):
    count = len(STAGES)
    at = [0] * len(chunks)
    ready = [0.0] * len(chunks)
    now = link = die = 0.0
    order = []

    def heavy(k):
        return STAGES[at[k]][0] not in LINK and STAGES[at[k]][0] != "F"

    def rank(k):
        name = STAGES[at[k]][0]
        if not heavy(k):
            return (0, 0, -at[k], k)
        return (2 if name == "Y" else 1, 0 if at[k] < 2 else 1, -at[k], k)

    while min(at) < count:
        todo = [k for k in range(len(chunks)) if at[k] < count]
        can = [k for k in todo if ready[k] <= now + 1e-9]
        if not can:
            now = min(ready[k] for k in todo)
            continue
        pick = min(can, key=rank)
        if heavy(pick) and link - now < 2 * LOOK_AHEAD:
            soon = [k for k in todo if not heavy(k) and ready[k] <= now + LOOK_AHEAD]
            if soon:
                pick = min(soon, key=lambda k: ready[k])
                now = ready[pick]
        name, cost = STAGES[at[pick]]
        size = chunks[pick] / 2
        now += cost * size + 0.8 + (2 if size < 1 and name == "MLP" else 0)
        order.append(pick)
        ready[pick] = now
        if name in LINK:
            link = max(link, now) + LINK[name] * size
            ready[pick] = link + 3
        elif name in DIE:
            die = max(die, now) + DIE[name] * size
            ready[pick] = die + 1.5
        at[pick] += 1
    return order


def rms_norm(rows, gain):
    rows32 = rows.astype(jnp.float32)
    inv_rms = lax.rsqrt(jnp.mean(rows32 * rows32, axis=-1, keepdims=True) + EPS)
    return (rows32 * inv_rms * gain.astype(jnp.float32)).astype(jnp.bfloat16)


def rope_tables(seq_len, head_dim):
    inv_freq = ROPE_BASE ** (-jnp.arange(0, head_dim, 2).astype(jnp.float32) / head_dim)
    angles = jnp.arange(seq_len).astype(jnp.float32)[:, None] * inv_freq[None, :]
    cos_tab = jnp.repeat(jnp.cos(angles), 2, axis=-1)
    sin_half = jnp.sin(angles)
    sin_tab = jnp.stack([-sin_half, sin_half], axis=-1).reshape(seq_len, head_dim)
    return cos_tab, sin_tab


def attend_kernel(heads, lens_ref, place_ref, q_ref, kv_ref, cos_ref, sin_ref, w_ref, k_ref, v_ref, own_ref, other_ref, rows_ref, turned_ref, w_vmem, sem):
    seq_len, head_dim = cos_ref.shape
    load = pltpu.make_async_copy(w_ref, w_vmem, sem)
    load.start()
    even = lax.broadcasted_iota(jnp.int32, (seq_len, head_dim), 1) % 2 == 0
    row_at = lax.broadcasted_iota(jnp.int32, (seq_len, head_dim), 0)
    query_at = lax.broadcasted_iota(jnp.int32, (seq_len, seq_len), 0)
    key_at = lax.broadcasted_iota(jnp.int32, (seq_len, seq_len), 1)
    cos_tab, sin_tab = cos_ref[...], sin_ref[...]

    def rotary(vecs):
        partner = jnp.where(even, pltpu.roll(vecs, head_dim - 1, 1), pltpu.roll(vecs, 1, 1))
        return vecs * cos_tab + partner * sin_tab

    for seq in range(k_ref.shape[0] // seq_len):
        here = slice(seq * seq_len, (seq + 1) * seq_len)
        length = lens_ref[seq]
        valid = row_at < length
        keys = jnp.where(valid, rotary(kv_ref[here, :head_dim]), 0.0).astype(jnp.bfloat16)
        values = jnp.where(valid, kv_ref[here, head_dim:], 0.0).astype(jnp.bfloat16)
        k_ref[here] = keys
        v_ref[here] = values
        allowed = (key_at <= query_at) & (key_at < length)
        for head in range(heads):
            cols = slice(head * head_dim, (head + 1) * head_dim)
            query = rotary(q_ref[here, cols]).astype(jnp.bfloat16)
            scores = lax.dot_general(query, keys, (((1,), (1,)), ((), ())), preferred_element_type=jnp.float32) * head_dim ** -0.5
            scores = jnp.where(allowed, scores, -jnp.inf)
            weights = jnp.exp(scores - jnp.max(scores, axis=-1, keepdims=True))
            probs = (weights / jnp.sum(weights, axis=-1, keepdims=True)).astype(jnp.bfloat16)
            rows_ref[here, cols] = jnp.dot(probs, values, preferred_element_type=jnp.float32)
    total = rows_ref.shape[0]
    chips = TP_CHIPS
    block = total // (CORES * chips)
    for c in range(CORES):
        for j in range(chips):
            core = lax.rem(place_ref[1] + c, CORES)
            chip = lax.rem(place_ref[0] + j, chips)
            source = pl.multiple_of((core * chips + chip) * block, block)
            at = (c * chips + j) * block
            turned_ref[at:at + block] = rows_ref[pl.ds(source, block)].astype(jnp.bfloat16)
    load.wait()
    width = w_ref.shape[1]
    step = min(width, 512)
    for n in range(0, width, step):
        part = jnp.dot(turned_ref[...], w_vmem[:, n:n + step], preferred_element_type=jnp.float32).astype(jnp.bfloat16)
        own_ref[:, n:n + step] = part[:total // 2]
        other_ref[:, n:n + step] = part[total // 2:]


def attend(lens, place, queries, kv, cos_tab, sin_tab, w_out):
    seq_len, head_dim = cos_tab.shape
    rows, q_width = queries.shape
    heads = q_width // head_dim
    width = w_out.shape[1]
    smem = pl.BlockSpec(memory_space=pltpu.SMEM)
    vmem = pl.BlockSpec(memory_space=pltpu.VMEM)
    return pl.pallas_call(
        functools.partial(attend_kernel, heads),
        in_specs=[smem, smem, vmem, vmem, vmem, vmem, pl.BlockSpec(memory_space=pl.ANY)],
        out_specs=[vmem, vmem, vmem, vmem],
        out_shape=[
            jax.ShapeDtypeStruct((rows, head_dim), jnp.bfloat16),
            jax.ShapeDtypeStruct((rows, head_dim), jnp.bfloat16),
            jax.ShapeDtypeStruct((rows // 2, width), jnp.bfloat16),
            jax.ShapeDtypeStruct((rows // 2, width), jnp.bfloat16),
        ],
        scratch_shapes=[
            pltpu.VMEM((rows, q_width), jnp.float32),
            pltpu.VMEM((rows, q_width), jnp.bfloat16),
            pltpu.VMEM(w_out.shape, jnp.bfloat16),
            pltpu.SemaphoreType.DMA,
        ],
        compiler_params=pltpu.CompilerParams(vmem_limit_bytes=40 * 2**20),
        cost_estimate=pl.CostEstimate(flops=4 * rows * seq_len * q_width + 2 * rows * q_width * width, bytes_accessed=2 * q_width * width + 2 * rows * width, transcendentals=rows * seq_len * heads),
    )(lens, place, queries, kv, cos_tab, sin_tab, w_out)


def mlp_kernel(count, *refs):
    blocks, (gate_ref, up_ref, down_ref, own_ref, other_ref, rows_ref, total_ref, sem) = refs[:count], refs[count:]
    tile = pl.program_id(0)

    @pl.when(tile == 0)
    def _():
        copies, at = [], 0
        for i, ref in enumerate(blocks):
            copies.append(pltpu.make_async_copy(ref, rows_ref.at[pl.ds(at, ref.shape[0])], sem.at[i]))
            at += ref.shape[0]
        for copy in copies:
            copy.start()
        for copy in copies:
            copy.wait()

    rows = rows_ref[...]
    gate = jnp.dot(rows, gate_ref[...], preferred_element_type=jnp.float32)
    up = jnp.dot(rows, up_ref[...], preferred_element_type=jnp.float32)
    gated = (gate * jax.nn.sigmoid(gate) * up).astype(jnp.bfloat16)
    width = down_ref.shape[1]
    half = rows_ref.shape[0] // 2
    step = min(width, 512)
    last = pl.num_programs(0) - 1

    def column(n, handle):
        cols = slice(n, n + step)
        handle(cols, jnp.dot(gated, down_ref[:, cols], preferred_element_type=jnp.float32))

    @pl.when(tile == 0)
    def _():
        for n in range(0, width, step):
            def first(cols, part):
                total_ref[:, cols] = part

            column(n, first)

    @pl.when((tile > 0) & (tile < last))
    def _():
        for n in range(0, width, step):
            def middle(cols, part):
                total_ref[:, cols] += part

            column(n, middle)

    @pl.when(tile == last)
    def _():
        for n in range(0, width, step):
            def final(cols, part):
                done = (total_ref[:, cols] + part).astype(jnp.bfloat16)
                own_ref[:, cols] = done[:half]
                other_ref[:, cols] = done[half:]

            column(n, final)


def mlp(blocks, w_gate, w_up, w_down, tile=256):
    width, hidden = w_gate.shape
    rows = sum(block.shape[0] for block in blocks)
    half = pl.BlockSpec((rows // 2, width), lambda i: (0, 0))
    return pl.pallas_call(
        functools.partial(mlp_kernel, len(blocks)),
        grid=(hidden // tile,),
        in_specs=[pl.BlockSpec(memory_space=pl.ANY)] * len(blocks) + [pl.BlockSpec((width, tile), lambda i: (0, i))] * 2 + [pl.BlockSpec((tile, width), lambda i: (i, 0))],
        out_specs=[half, half],
        out_shape=[jax.ShapeDtypeStruct((rows // 2, width), jnp.bfloat16)] * 2,
        scratch_shapes=[
            pltpu.VMEM((rows, width), jnp.bfloat16),
            pltpu.VMEM((rows, width), jnp.float32),
            pltpu.SemaphoreType.DMA((len(blocks),)),
        ],
        compiler_params=pltpu.CompilerParams(dimension_semantics=("arbitrary",), vmem_limit_bytes=60 * 2**20),
        cost_estimate=pl.CostEstimate(flops=6 * rows * width * hidden, bytes_accessed=6 * width * hidden + 4 * rows * width, transcendentals=rows * hidden),
    )(*blocks, w_gate, w_up, w_down)


def place_kernel(count, offsets_ref, *refs):
    blocks, (out_ref, buffer, sems) = refs[:count], refs[-3:]
    loads, stores, at = [], [], 0
    for i, ref in enumerate(blocks):
        size = ref.shape[0]
        here = buffer.at[pl.ds(at, size)]
        there = out_ref.at[pl.ds(pl.multiple_of(offsets_ref[i], 16), size)]
        loads.append(pltpu.make_async_copy(ref, here, sems.at[i]))
        stores.append(pltpu.make_async_copy(here, there, sems.at[count + i]))
        at += size
    for copy in loads:
        copy.start()
    for load, store in zip(loads, stores):
        load.wait()
        store.start()
    for copy in stores:
        copy.wait()


def place_blocks(offsets, blocks, result, total):
    count = len(blocks)
    rows, width = sum(block.shape[0] for block in blocks), blocks[0].shape[1]
    hbm = pl.BlockSpec(memory_space=pl.ANY)
    held = () if result is None else (result,)
    return pl.pallas_call(
        functools.partial(place_kernel, count),
        in_specs=[pl.BlockSpec(memory_space=pltpu.SMEM)] + [hbm] * (count + len(held)),
        out_specs=hbm,
        out_shape=jax.ShapeDtypeStruct((total, width), jnp.bfloat16),
        scratch_shapes=[pltpu.VMEM((rows, width), jnp.bfloat16), pltpu.SemaphoreType.DMA((2 * count,))],
        input_output_aliases={count + 1: 0} if held else {},
        cost_estimate=pl.CostEstimate(flops=2 * rows * width * 1024, bytes_accessed=4 * rows * width, transcendentals=0),
    )(offsets, *blocks, *held)


def solution(mesh):
    tp_size = mesh.shape["tp"]
    chips = tp_size // CORES
    to_left = [(i, (i - CORES) % tp_size) for i in range(tp_size)]
    to_right = [(i, (i + CORES) % tp_size) for i in range(tp_size)]
    to_sibling = [(i, i ^ 1) for i in range(tp_size)]

    def send(array, perm):
        return lax.ppermute(array, "tp", perm)

    def layer_body(x, seq_lens, w_query, w_key, w_value, w_out, w_gate, w_up, w_down, attn_gain, mlp_gain, k_cache, v_cache):
        batch_size, seq_len, model_width = x.shape
        head_dim = k_cache.shape[3]
        tp_index = lax.axis_index("tp")
        chip, core = tp_index // CORES, tp_index % CORES
        cos_tab, sin_tab = rope_tables(seq_len, head_dim)
        w_kv = jnp.concatenate([w_key, w_value], axis=1)
        x_flat = x.reshape(batch_size * seq_len, model_width)
        place = jnp.stack([chip, core]).astype(jnp.int32)
        state = {"last": w_kv, "y": None}
        keys_all, values_all = [None] * len(CHUNKS), [None] * len(CHUNKS)

        def after(*arrays):
            return lax.optimization_barrier((*arrays, state["last"]))[:-1]

        def dot(rows, weight):
            return jnp.dot(rows, weight, preferred_element_type=jnp.float32)

        def exchange(own, other, resid):
            half = own.shape[0] // (2 * chips)
            got = send(other, to_sibling)
            yield
            own, got = after(own, got)

            def pair(j, k):
                rows = slice((2 * j + k) * half, (2 * j + k + 1) * half)
                return own[rows].astype(jnp.float32) + got[rows].astype(jnp.float32)

            go_left = jnp.concatenate([pair(2, 0), pair(3, 1)], axis=0)
            go_right = jnp.concatenate([pair(2, 1), pair(1, 0)], axis=0)
            state["last"] = go_right
            from_right, from_left = send(go_left, to_left), send(go_right, to_right)
            yield
            own, got, from_right, from_left = after(own, got, from_right, from_left)
            go_left = pair(3, 0) + from_right[:half]
            go_right = pair(1, 1) + from_left[:half]
            state["last"] = go_right
            far_right, far_left = send(go_left, to_left), send(go_right, to_right)
            yield
            own, got, from_right, from_left, far_right, far_left = after(own, got, from_right, from_left, far_right, far_left)
            total = jnp.concatenate([pair(0, 0) + from_left[half:] + far_right, pair(0, 1) + from_right[half:] + far_left], axis=0)
            return (resid.astype(jnp.float32) + total).astype(jnp.bfloat16)

        def gather(block):
            half = block.shape[0] // 2
            state["last"] = block
            right, left = send(block, to_left), send(block, to_right)
            block_other = send(block, to_sibling)
            yield
            right, left = after(right, left)
            go_left, go_right = right[:half], left[half:]
            state["last"] = go_right
            far_right, far_left = send(go_left, to_left), send(go_right, to_right)
            right_other, left_other = send(right, to_sibling), send(left, to_sibling)
            yield
            own = [block, right, far_right, far_left, left]
            return own, [block_other, right_other, send(far_right, to_sibling), send(far_left, to_sibling), left_other]

        def chunk_stages(index):
            first, count = sum(CHUNKS[:index]) * seq_len, CHUNKS[index]
            rows = count * seq_len
            block = rows // tp_size
            (start,) = after(jnp.int32(first))
            x_c = lax.dynamic_slice(x_flat, (start, 0), (rows, model_width))
            normed = rms_norm(x_c, attn_gain)
            queries, kv = dot(normed, w_query), dot(normed, w_kv)
            state["last"] = kv
            yield
            queries, kv = after(queries, kv)
            lens = seq_lens[first // seq_len:first // seq_len + count]
            keys, values, own, other = attend(lens, place, queries, kv, cos_tab, sin_tab, w_out)
            keys_all[index], values_all[index] = keys, values
            state["last"] = other
            resid = lax.dynamic_slice(x_flat, (first + core * (rows // CORES) + chip * block, 0), (block, model_width))
            hidden = yield from exchange(own, other, resid)
            own, other = yield from gather(rms_norm(hidden, mlp_gain))
            yield
            blocks = after(*own, *other)
            own, other = mlp(blocks, w_gate, w_up, w_down)
            state["last"] = other
            out = yield from exchange(own, other, hidden)
            own, other = yield from gather(out)
            yield
            blocks = after(*own, *other)
            offsets = []
            for parity in (core, 1 - core):
                for j, shift in ((0, 0), (1, 0), (2, 0), (2, block // 2), (3, 0)):
                    offsets.append(first + parity * (rows // CORES) + (chip + j) % chips * block + shift)
            state["y"] = state["last"] = place_blocks(jnp.stack(offsets), blocks, state["y"], x_flat.shape[0])

        runs = [chunk_stages(index) for index in range(len(CHUNKS))]
        for index in stage_order(CHUNKS):
            next(runs[index], None)
        y = state["y"].reshape(x.shape)
        keys = jnp.concatenate(keys_all, axis=0).reshape(batch_size, seq_len, 1, head_dim)
        values = jnp.concatenate(values_all, axis=0).reshape(batch_size, seq_len, 1, head_dim)
        k_cache_out = lax.dynamic_update_slice(k_cache, keys, (0, 0, 0, 0))
        v_cache_out = lax.dynamic_update_slice(v_cache, values, (0, 0, 0, 0))
        return y, k_cache_out, v_cache_out

    cache_spec = P("dp", None, "tp", None)
    return jax.shard_map(layer_body, mesh=mesh, in_specs=(P("dp", None, None), P("dp"), P(None, "tp"), P(None, "tp"), P(None, "tp"), P("tp", None), P(None, "tp"), P(None, "tp"), P("tp", None), P(), P(), cache_spec, cache_spec), out_specs=(P("dp", None, None), cache_spec, cache_spec), check_vma=False)
```

time: 1230 us -> 1050 us (0.85)
  Pallas kernels: 0 us -> 308 us
  blocking collectives: 278 us -> 0 us
  matrix products: 277 us -> 66.8 us
  waiting for transfers between devices: 510 us -> 337 us
  starting transfers between devices: 8.52 us -> 158 us
  other arithmetic: 66.9 us -> 118 us
  local copies, waits for them, and re-layouts: 67.2 us -> 51.3 us
    ppermute x0 -> x140, waiting for transfers between devices: none -> 337 us  [send(): return lax.ppermute(array, 'tp', perm)]
    pallas_call x0 -> x15, Pallas kernels: none -> 308 us  [the longest x5 230 us: mlp(): pl.pallas_call(functools.partial(mlp_kernel, len(blocks)), grid=(hidden /...]
    all_to_all x1 -> x0, blocking collectives: 278 us -> none  [sum_partials(): received = lax.all_to_all(stacked, 'tp', 1, 1, tiled=True)]
    all_to_all x1 -> x0, waiting for transfers between devices: 273 us -> none  [sum_partials(): received = lax.all_to_all(stacked, 'tp', 1, 1, tiled=True)]
    all_gather x2 -> x0, waiting for transfers between devices: 237 us -> none  [the longest x1 119 us: layer_shard(): lax.all_gather(rms_norm(hidden_rows, mlp_gain), 'tp', axis=1, tiled=True)]
    dot_general x9 -> x10, matrix products: 277 us -> 66.8 us  [dot(): return jnp.dot(rows, weight, preferred_element_type=jnp.float32)]
    ppermute x0 -> x140, starting transfers between devices: none -> 158 us  [send(): return lax.ppermute(array, 'tp', perm)]
    add x0 -> x30, other arithmetic: none -> 59.6 us  [the longest x10 18.7 us: exchange(): pair(0, 0) + from_left[half:] + far_right]
  transfers between devices with their start and end apart: 3 -> 140, of which waited for: 3 -> 32; matrix products, arithmetic and copies ran while one was open for 0% -> 17% of each run, Pallas kernels for 0% -> 19%
where the time goes in v1:
time: 1050 us; the launch traced here: 1040 us
  waiting for transfers between devices  337 us (32%)
  Pallas kernels  308 us (29%)
  starting transfers between devices  158 us (15%)
  other arithmetic  118 us (11%)
  matrix products  66.8 us (6%)
  local copies, waits for them, and re-layouts  51.3 us (5%)
    ppermute x140, waiting for transfers between devices, send(): return lax.ppermute(array, 'tp', perm)  337 us
    pallas_call x5, Pallas kernels, mlp(): pl.pallas_call(functools.partial(mlp_kernel, len(blocks)), grid=(hidden /...  230 us
    ppermute x140, starting transfers between devices, send(): return lax.ppermute(array, 'tp', perm)  158 us
    dot_general x10, matrix products, dot(): return jnp.dot(rows, weight, preferred_element_type=jnp.float32)  66.8 us
    pallas_call x5, Pallas kernels, attend(): pl.pallas_call(functools.partial(attend_kernel, heads), in_specs=[smem, s...  51.8 us
    pallas_call x5, Pallas kernels, place_blocks(): pl.pallas_call(functools.partial(place_kernel, count), in_specs=[pl.Block...  25.9 us
    unnamed x296, local copies, waits for them, and re-layouts  25.6 us
    reduce_sum x10, other arithmetic, rms_norm(): inv_rms = lax.rsqrt(jnp.mean(rows32 * rows32, axis=-1, keepdims=True) + EPS)  24.6 us
  transfers between devices with their start and end apart: 140, of which 32 were waited for; matrix products, arithmetic and copies ran while one was open for 17% of the time, Pallas kernels for 19%

profile of v1, /device:TPU:81, one launch (start us, length us, event | category | flops | bytes accessed | tf_op | source)
XLA Modules:
  0.0 1041.6 jit_solution(16856874738950617904)
XLA Ops:
  7.2 3.9 fusion.56.kv_ref
  11.1 7.3 fusion.58.q_ref
  23.3 7.6 shard_map.148
  38.5 4.2 fusion
  42.7 5.7 fusion.38.kv_ref
  48.8 8.1 fusion.40.q_ref
  57.0 12.3 %shard_map.149 = (bf16[512,128]{1,0:T(8,128)(2,1)S(1)}, bf16[512,128]{1,0:T(8,128)(2,1)S(1)}, bf16[256,6144]{1,0:T(8,128)(2,1)S(1)}, bf16[256,6144]{1,0:T(8,128)(2,1)}) custom-call(s32[2]{0:T(128)S(1)} %get-tuple-element.666.lens_ref, s32[2]{0:T(128)S(1)} %pad_add_fusion.place_ref, f32[512,768]{1,0:T(8,128)S(1)} %fusion.40.q_ref, ...), custom_call_target="tpu_custom_call" | custom-call | flops 5234491392 | bytes 15728640 | tf_op jit(solution)/shard_map/pallas_call | solution.py:138
  75.1 15.9 %collective-permute-done.2 = f32[32,6144]{1,0:T(8,128)} collective-permute-done((f32[32,6144]{1,0:T(8,128)}, f32[32,6144]{1,0:T(8,128)}, u32[]{:S(2)}, u32[]{:S(2)}) %collective-permute-start.2) | collective-permute-done | bytes 786464 | tf_op jit(solution)/shard_map/ppermute | solution.py:277
  102.1 4.1 fusion.3
  106.2 9.7 fusion.36.q_ref
  116.0 5.6 fusion.34.kv_ref
  125.5 12.3 %shard_map.150 = (bf16[512,128]{1,0:T(8,128)(2,1)S(1)}, bf16[512,128]{1,0:T(8,128)(2,1)S(1)}, bf16[256,6144]{1,0:T(8,128)(2,1)S(1)}, bf16[256,6144]{1,0:T(8,128)(2,1)}) custom-call(s32[2]{0:T(128)S(1)} %get-tuple-element.667.lens_ref, s32[2]{0:T(128)S(1)} %pad_add_fusion.place_ref, f32[512,768]{1,0:T(8,128)S(1)} %fusion.36.q_ref, ...), custom_call_target="tpu_custom_call" | custom-call | flops 5234491392 | bytes 15728640 | tf_op jit(solution)/shard_map/pallas_call | solution.py:138
  146.9 32.5 %collective-permute-done.4 = f32[64,6144]{1,0:T(8,128)} collective-permute-done((f32[64,6144]{1,0:T(8,128)}, f32[64,6144]{1,0:T(8,128)}, u32[]{:S(2)}, u32[]{:S(2)}) %collective-permute-start.4) | collective-permute-done | bytes 1572896 | tf_op jit(solution)/shard_map/ppermute | solution.py:277
  190.1 4.1 fusion.6
  194.2 9.5 fusion.32.q_ref
  203.7 5.6 fusion.30.kv_ref
  210.9 12.3 %shard_map.151 = (bf16[512,128]{1,0:T(8,128)(2,1)S(1)}, bf16[512,128]{1,0:T(8,128)(2,1)S(1)}, bf16[256,6144]{1,0:T(8,128)(2,1)S(1)}, bf16[256,6144]{1,0:T(8,128)(2,1)}) custom-call(s32[2]{0:T(128)S(1)} %get-tuple-element.665.lens_ref, s32[2]{0:T(128)S(1)} %pad_add_fusion.place_ref, f32[512,768]{1,0:T(8,128)S(1)} %fusion.32.q_ref, ...), custom_call_target="tpu_custom_call" | custom-call | flops 5234491392 | bytes 15728640 | tf_op jit(solution)/shard_map/pallas_call | solution.py:138
  239.7 4.0 fusion.52.kv_ref
  243.8 7.4 fusion.54.q_ref
  255.4 7.3 shard_map.152
  264.3 6.8 collective-permute-done.15
  284.8 35.1 %shard_map.153 = (bf16[128,6144]{1,0:T(8,128)(2,1)}, bf16[128,6144]{1,0:T(8,128)(2,1)}) custom-call(bf16[32,6144]{1,0:T(8,128)(2,1)} %fusion.44.refs_0_, bf16[32,6144]{1,0:T(8,128)(2,1)} %collective-permute-done.11.refs_1_, bf16[16,6144]{1,0:T(8,128)(2,1)} %copy-done.107, bf16[16,6144]{1,0:T(8,128)(2,1)} %copy-done.105, ...), custom_call_target="tpu_custom_call" | custom-call | flops 19327352832 | bytes 81788928 | tf_op jit(solution)/shard_map/pallas_call | solution.py:218
  326.0 14.9 %collective-permute-done.31.refs_1_ = bf16[64,6144]{1,0:T(8,128)(2,1)} collective-permute-done((bf16[64,6144]{1,0:T(8,128)(2,1)}, bf16[64,6144]{1,0:T(8,128)(2,1)}, u32[]{:S(2)}, u32[]{:S(2)}) %collective-permute-start.31) | collective-permute-done | bytes 786464 | tf_op jit(solution)/shard_map/ppermute | solution.py:277
  350.3 27.5 %collective-permute-done.21 = f32[64,6144]{1,0:T(8,128)S(1)} collective-permute-done((f32[64,6144]{1,0:T(8,128)S(1)}, f32[64,6144]{1,0:T(8,128)S(1)}, u32[]{:S(2)}, u32[]{:S(2)}) %collective-permute-start.21) | collective-permute-done | bytes 1572896 | tf_op jit(solution)/shard_map/ppermute | solution.py:277
  382.3 12.3 %collective-permute-done.19 = f32[32,6144]{1,0:T(8,128)S(1)} collective-permute-done((f32[32,6144]{1,0:T(8,128)S(1)}, f32[32,6144]{1,0:T(8,128)S(1)}, u32[]{:S(2)}, u32[]{:S(2)}) %collective-permute-start.19) | collective-permute-done | bytes 786464 | tf_op jit(solution)/shard_map/ppermute | solution.py:277
  403.1 16.8 %collective-permute-done.37.refs_2_ = bf16[32,6144]{1,0:T(8,128)(2,1)S(1)} collective-permute-done((bf16[32,6144]{1,0:T(8,128)(2,1)S(1)}, bf16[32,6144]{1,0:T(8,128)(2,1)S(1)}, u32[]{:S(2)}, u32[]{:S(2)}) %collective-permute-start.37) | collective-permute-done | bytes 393248 | tf_op jit(solution)/shard_map/ppermute | solution.py:277
  434.8 53.4 %shard_map.154 = (bf16[256,6144]{1,0:T(8,128)(2,1)}, bf16[256,6144]{1,0:T(8,128)(2,1)}) custom-call(bf16[64,6144]{1,0:T(8,128)(2,1)} %fusion.17.refs_0_, bf16[64,6144]{1,0:T(8,128)(2,1)} %collective-permute-done.31.refs_1_, bf16[32,6144]{1,0:T(8,128)(2,1)} %copy-done.128, bf16[32,6144]{1,0:T(8,128)(2,1)} %copy-done.126, ...), custom_call_target="tpu_custom_call" | custom-call | flops 38654705664 | bytes 88080384 | tf_op jit(solution)/shard_map/pallas_call | solution.py:218
  494.2 12.2 %collective-permute-done.47 = f32[32,6144]{1,0:T(8,128)S(1)} collective-permute-done((f32[32,6144]{1,0:T(8,128)}, f32[32,6144]{1,0:T(8,128)S(1)}, u32[]{:S(2)}, u32[]{:S(2)}) %collective-permute-start.47) | collective-permute-done | bytes 786464 | tf_op jit(solution)/shard_map/ppermute | solution.py:277
  529.4 4.0 collective-permute-start.56
  542.0 53.5 %shard_map.155 = (bf16[256,6144]{1,0:T(8,128)(2,1)}, bf16[256,6144]{1,0:T(8,128)(2,1)}) custom-call(bf16[64,6144]{1,0:T(8,128)(2,1)} %fusion.21.refs_0_, bf16[64,6144]{1,0:T(8,128)(2,1)} %collective-permute-done.49.refs_1_, bf16[32,6144]{1,0:T(8,128)(2,1)} %copy-done.130, bf16[32,6144]{1,0:T(8,128)(2,1)} %copy-done.129, ...), custom_call_target="tpu_custom_call" | custom-call | flops 38654705664 | bytes 88080384 | tf_op jit(solution)/shard_map/pallas_call | solution.py:218
  601.9 30.9 %collective-permute-done.65 = f32[64,6144]{1,0:T(8,128)S(1)} collective-permute-done((f32[64,6144]{1,0:T(8,128)S(1)}, f32[64,6144]{1,0:T(8,128)S(1)}, u32[]{:S(2)}, u32[]{:S(2)}) %collective-permute-start.65) | collective-permute-done | bytes 1572896 | tf_op jit(solution)/shard_map/ppermute | solution.py:277
  637.6 12.2 %collective-permute-done.63.refs_1_ = bf16[64,6144]{1,0:T(8,128)(2,1)S(1)} collective-permute-done((bf16[64,6144]{1,0:T(8,128)(2,1)}, bf16[64,6144]{1,0:T(8,128)(2,1)S(1)}, u32[]{:S(2)}, u32[]{:S(2)}) %collective-permute-start.63) | collective-permute-done | bytes 786464 | tf_op jit(solution)/shard_map/ppermute | solution.py:277
  653.1 5.1 collective-permute-done.61.refs_1_
  674.0 17.7 %collective-permute-done.74.refs_2_ = bf16[32,6144]{1,0:T(8,128)(2,1)S(1)} collective-permute-done((bf16[32,6144]{1,0:T(8,128)(2,1)S(1)}, bf16[32,6144]{1,0:T(8,128)(2,1)S(1)}, u32[]{:S(2)}, u32[]{:S(2)}) %collective-permute-start.74) | collective-permute-done | bytes 393248 | tf_op jit(solution)/shard_map/ppermute | solution.py:277
  705.1 53.2 %shard_map.156 = (bf16[256,6144]{1,0:T(8,128)(2,1)}, bf16[256,6144]{1,0:T(8,128)(2,1)}) custom-call(bf16[64,6144]{1,0:T(8,128)(2,1)} %fusion.25.refs_0_, bf16[64,6144]{1,0:T(8,128)(2,1)} %copy-done.111, bf16[32,6144]{1,0:T(8,128)(2,1)} %copy-done.131, bf16[32,6144]{1,0:T(8,128)(2,1)} %copy-done.127, bf16[64,6144]{1,0:T(8,128)(2,1)} %copy-done.112, ...), custom_call_target="tpu_custom_call" | custom-call | flops 38654705664 | bytes 88080384 | tf_op jit(solution)/shard_map/pallas_call | solution.py:218
  759.4 6.2 collective-permute-done.86.refs_2_
  765.7 6.9 collective-permute-done.87.refs_3_
  789.5 7.9 collective-permute-done.84.refs_1_
  814.0 35.1 %shard_map.158 = (bf16[128,6144]{1,0:T(8,128)(2,1)}, bf16[128,6144]{1,0:T(8,128)(2,1)}) custom-call(bf16[32,6144]{1,0:T(8,128)(2,1)} %fusion.48.refs_0_, bf16[32,6144]{1,0:T(8,128)(2,1)} %copy-done.67, bf16[16,6144]{1,0:T(8,128)(2,1)} %collective-permute-done.67.refs_2_, bf16[16,6144]{1,0:T(8,128)(2,1)} %copy-done.103, bf16[32,6144]{1,0:T(8,128)(2,1)} %copy-done.68, ...), custom_call_target="tpu_custom_call" | custom-call | flops 19327352832 | bytes 81788928 | tf_op jit(solution)/shard_map/pallas_call | solution.py:218
  869.6 6.3 shard_map.159.refs_10_
  876.0 21.2 %collective-permute-done.102 = f32[64,6144]{1,0:T(8,128)} collective-permute-done((f32[64,6144]{1,0:T(8,128)}, f32[64,6144]{1,0:T(8,128)}, u32[]{:S(2)}, u32[]{:S(2)}) %collective-permute-start.102) | collective-permute-done | bytes 1572896 | tf_op jit(solution)/shard_map/ppermute | solution.py:277
  903.6 10.4 collective-permute-done.100.refs_1_
  919.6 12.2 %collective-permute-done.99 = f32[32,6144]{1,0:T(8,128)S(1)} collective-permute-done((f32[32,6144]{1,0:T(8,128)}, f32[32,6144]{1,0:T(8,128)S(1)}, u32[]{:S(2)}, u32[]{:S(2)}) %collective-permute-start.99) | collective-permute-done | bytes 786464 | tf_op jit(solution)/shard_map/ppermute | solution.py:277
  935.5 20.5 %collective-permute-done.113.refs_2_ = bf16[32,6144]{1,0:T(8,128)(2,1)S(1)} collective-permute-done((bf16[32,6144]{1,0:T(8,128)(2,1)S(1)}, bf16[32,6144]{1,0:T(8,128)(2,1)S(1)}, u32[]{:S(2)}, u32[]{:S(2)}) %collective-permute-start.113) | collective-permute-done | bytes 393248 | tf_op jit(solution)/shard_map/ppermute | solution.py:277
  968.5 6.3 shard_map.160.refs_10_
  974.9 14.9 %collective-permute-done.111 = f32[16,6144]{1,0:T(8,128)} collective-permute-done((f32[16,6144]{1,0:T(8,128)}, f32[16,6144]{1,0:T(8,128)}, u32[]{:S(2)}, u32[]{:S(2)}) %collective-permute-start.111) | collective-permute-done | bytes 393248 | tf_op jit(solution)/shard_map/ppermute | solution.py:277
  1021.3 5.9 collective-permute-done.127.refs_3_
  1030.6 6.3 shard_map.161.refs_10_
  (681 shorter events, 343.7 us)
Async XLA Ops:
  102.1 44.8 %collective-permute-start.5 = (f32[64,6144]{1,0:T(8,128)}, f32[64,6144]{1,0:T(8,128)}, u32[]{:S(2)}, u32[]{:S(2)}) collective-permute-start(f32[64,6144]{1,0:T(8,128)} %pad_maximum_fusion.1), channel_id=1, source_target_pairs={{0,2},{1,3},{2,4},{3,5},{4,6},{5,7},{6,0},{7,1},{8,10},{9,11},{10,... | collective-permute-start | bytes 4718600 | tf_op jit(solution)/shard_map/ppermute | solution.py:277
  139.1 47.0 %collective-permute-start.10 = (bf16[256,6144]{1,0:T(8,128)(2,1)}, bf16[256,6144]{1,0:T(8,128)(2,1)}, u32[]{:S(2)}, u32[]{:S(2)}) collective-permute-start(bf16[256,6144]{1,0:T(8,128)(2,1)} %get-tuple-element.315), channel_id=1, source_target_pairs={{0,1},{1,0},{2,3},{3,2},{4,5},{5,4},{6,7},{7,6},{8,9},{9,8},{10,11... | collective-permute-start | bytes 9437192 | tf_op jit(solution)/shard_map/ppermute | solution.py:277
  142.0 37.4 %collective-permute-start.4 = (f32[64,6144]{1,0:T(8,128)}, f32[64,6144]{1,0:T(8,128)}, u32[]{:S(2)}, u32[]{:S(2)}) collective-permute-start(f32[64,6144]{1,0:T(8,128)} %pad_maximum_fusion), channel_id=1, source_target_pairs={{0,6},{1,7},{2,0},{3,1},{4,2},{5,3},{6,4},{7,5},{8,14},{9,15},{10,... | collective-permute-start | bytes 4718600 | tf_op jit(solution)/shard_map/ppermute | solution.py:277
  145.4 63.9 %collective-permute-start.11 = (bf16[32,6144]{1,0:T(8,128)(2,1)}, bf16[32,6144]{1,0:T(8,128)(2,1)}, u32[]{:S(2)}, u32[]{:S(2)}) collective-permute-start(bf16[32,6144]{1,0:T(8,128)(2,1)} %fusion.44.refs_0_), channel_id=1, source_target_pairs={{0,6},{1,7},{2,0},{3,1},{4,2},{5,3},{6,4},{7,5},{8,14},{9,15},{10,... | collective-permute-start | bytes 1179656 | tf_op jit(solution)/shard_map/ppermute | solution.py:277
  145.6 63.8 %collective-permute-start.12 = (bf16[32,6144]{1,0:T(8,128)(2,1)}, bf16[32,6144]{1,0:T(8,128)(2,1)}, u32[]{:S(2)}, u32[]{:S(2)}) collective-permute-start(bf16[32,6144]{1,0:T(8,128)(2,1)} %fusion.44.refs_0_), channel_id=1, source_target_pairs={{0,2},{1,3},{2,4},{3,5},{4,6},{5,7},{6,0},{7,1},{8,10},{9,11},{10,... | collective-permute-start | bytes 1179656 | tf_op jit(solution)/shard_map/ppermute | solution.py:277
  182.6 42.6 %collective-permute-start.8 = (f32[32,6144]{1,0:T(8,128)}, f32[32,6144]{1,0:T(8,128)}, u32[]{:S(2)}, u32[]{:S(2)}) collective-permute-start(f32[32,6144]{1,0:T(8,128)} %get-tuple-element.626), channel_id=1, source_target_pairs={{0,6},{1,7},{2,0},{3,1},{4,2},{5,3},{6,4},{7,5},{8,14},{9,15},{10,... | collective-permute-start | bytes 2359304 | tf_op jit(solution)/shard_map/ppermute | solution.py:277
  186.0 39.2 %collective-permute-start.9 = (f32[32,6144]{1,0:T(8,128)}, f32[32,6144]{1,0:T(8,128)}, u32[]{:S(2)}, u32[]{:S(2)}) collective-permute-start(f32[32,6144]{1,0:T(8,128)} %get-tuple-element.625), channel_id=1, source_target_pairs={{0,2},{1,3},{2,4},{3,5},{4,6},{5,7},{6,0},{7,1},{8,10},{9,11},{10,... | collective-permute-start | bytes 2359304 | tf_op jit(solution)/shard_map/ppermute | solution.py:277
  231.4 40.7 %collective-permute-start.16 = (f32[64,6144]{1,0:T(8,128)}, f32[64,6144]{1,0:T(8,128)}, u32[]{:S(2)}, u32[]{:S(2)}) collective-permute-start(f32[64,6144]{1,0:T(8,128)} %pad_maximum_fusion.2), channel_id=1, source_target_pairs={{0,2},{1,3},{2,4},{3,5},{4,6},{5,7},{6,0},{7,1},{8,10},{9,11},{10,... | collective-permute-start | bytes 4718600 | tf_op jit(solution)/shard_map/ppermute | solution.py:277
  234.0 37.1 %collective-permute-start.15 = (f32[64,6144]{1,0:T(8,128)}, f32[64,6144]{1,0:T(8,128)}, u32[]{:S(2)}, u32[]{:S(2)}) collective-permute-start(f32[64,6144]{1,0:T(8,128)} %pad_maximum_fusion.4), channel_id=1, source_target_pairs={{0,6},{1,7},{2,0},{3,1},{4,2},{5,3},{6,4},{7,5},{8,14},{9,15},{10,... | collective-permute-start | bytes 4718600 | tf_op jit(solution)/shard_map/ppermute | solution.py:277
  323.8 102.3 %collective-permute-start.39 = (bf16[64,6144]{1,0:T(8,128)(2,1)}, bf16[64,6144]{1,0:T(8,128)(2,1)S(1)}, u32[]{:S(2)}, u32[]{:S(2)}) collective-permute-start(bf16[64,6144]{1,0:T(8,128)(2,1)} %fusion.17.refs_0_), channel_id=1, source_target_pairs={{0,1},{1,0},{2,3},{3,2},{4,5},{5,4},{6,7},{7,6},{8,9},{9,8},{10,11... | collective-permute-start | bytes 2359304 | tf_op jit(solution)/shard_map/ppermute | solution.py:277
  324.3 54.3 %collective-permute-start.22 = (f32[64,6144]{1,0:T(8,128)}, f32[64,6144]{1,0:T(8,128)S(1)}, u32[]{:S(2)}, u32[]{:S(2)}) collective-permute-start(f32[64,6144]{1,0:T(8,128)} %pad_maximum_fusion.3), channel_id=1, source_target_pairs={{0,2},{1,3},{2,4},{3,5},{4,6},{5,7},{6,0},{7,1},{8,10},{9,11},{10,... | collective-permute-start | bytes 4718600 | tf_op jit(solution)/shard_map/ppermute | solution.py:277
  340.9 56.0 %collective-permute-start.20 = (f32[32,6144]{1,0:T(8,128)S(1)}, f32[32,6144]{1,0:T(8,128)S(1)}, u32[]{:S(2)}, u32[]{:S(2)}) collective-permute-start(f32[32,6144]{1,0:T(8,128)S(1)} %copy-done.79), channel_id=1, source_target_pairs={{0,2},{1,3},{2,4},{3,5},{4,6},{5,7},{6,0},{7,1},{8,10},{9,11},{10,... | collective-permute-start | bytes 2359304 | tf_op jit(solution)/shard_map/ppermute | solution.py:277
  344.0 33.8 %collective-permute-start.21 = (f32[64,6144]{1,0:T(8,128)S(1)}, f32[64,6144]{1,0:T(8,128)S(1)}, u32[]{:S(2)}, u32[]{:S(2)}) collective-permute-start(f32[64,6144]{1,0:T(8,128)S(1)} %pad_maximum_fusion.5), channel_id=1, source_target_pairs={{0,6},{1,7},{2,0},{3,1},{4,2},{5,3},{6,4},{7,5},{8,14},{9,15},{10,... | collective-permute-start | bytes 4718600 | tf_op jit(solution)/shard_map/ppermute | solution.py:277
  346.5 48.1 %collective-permute-start.19 = (f32[32,6144]{1,0:T(8,128)S(1)}, f32[32,6144]{1,0:T(8,128)S(1)}, u32[]{:S(2)}, u32[]{:S(2)}) collective-permute-start(f32[32,6144]{1,0:T(8,128)S(1)} %copy-done.80), channel_id=1, source_target_pairs={{0,6},{1,7},{2,0},{3,1},{4,2},{5,3},{6,4},{7,5},{8,14},{9,15},{10,... | collective-permute-start | bytes 2359304 | tf_op jit(solution)/shard_map/ppermute | solution.py:277
  377.8 45.4 %collective-permute-start.18 = (f32[32,6144]{1,0:T(8,128)S(1)}, f32[32,6144]{1,0:T(8,128)S(1)}, u32[]{:S(2)}, u32[]{:S(2)}) collective-permute-start(f32[32,6144]{1,0:T(8,128)S(1)} %copy-done.84), channel_id=1, source_target_pairs={{0,2},{1,3},{2,4},{3,5},{4,6},{5,7},{6,0},{7,1},{8,10},{9,11},{10,... | collective-permute-start | bytes 2359304 | tf_op jit(solution)/shard_map/ppermute | solution.py:277
  378.6 44.4 %collective-permute-start.38 = (bf16[32,6144]{1,0:T(8,128)(2,1)S(1)}, bf16[32,6144]{1,0:T(8,128)(2,1)S(1)}, u32[]{:S(2)}, u32[]{:S(2)}) collective-permute-start(bf16[32,6144]{1,0:T(8,128)(2,1)S(1)} %slice.752), channel_id=1, source_target_pairs={{0,2},{1,3},{2,4},{3,5},{4,6},{5,7},{6,0},{7,1},{8,10},{9,11},{10,... | collective-permute-start | bytes 1179656 | tf_op jit(solution)/shard_map/ppermute | solution.py:277
  426.1 63.4 %collective-permute-start.36 = (f32[32,6144]{1,0:T(8,128)}, f32[32,6144]{1,0:T(8,128)}, u32[]{:S(2)}, u32[]{:S(2)}) collective-permute-start(f32[32,6144]{1,0:T(8,128)} %pad_maximum_fusion.16), channel_id=1, source_target_pairs={{0,2},{1,3},{2,4},{3,5},{4,6},{5,7},{6,0},{7,1},{8,10},{9,11},{10,... | collective-permute-start | bytes 2359304 | tf_op jit(solution)/shard_map/ppermute | solution.py:277
  427.0 65.9 %collective-permute-start.49 = (bf16[64,6144]{1,0:T(8,128)(2,1)}, bf16[64,6144]{1,0:T(8,128)(2,1)}, u32[]{:S(2)}, u32[]{:S(2)}) collective-permute-start(bf16[64,6144]{1,0:T(8,128)(2,1)} %fusion.21.refs_0_), channel_id=1, source_target_pairs={{0,6},{1,7},{2,0},{3,1},{4,2},{5,3},{6,4},{7,5},{8,14},{9,15},{10,... | collective-permute-start | bytes 2359304 | tf_op jit(solution)/shard_map/ppermute | solution.py:277
  430.3 62.7 %collective-permute-start.50 = (bf16[64,6144]{1,0:T(8,128)(2,1)}, bf16[64,6144]{1,0:T(8,128)(2,1)}, u32[]{:S(2)}, u32[]{:S(2)}) collective-permute-start(bf16[64,6144]{1,0:T(8,128)(2,1)} %fusion.21.refs_0_), channel_id=1, source_target_pairs={{0,2},{1,3},{2,4},{3,5},{4,6},{5,7},{6,0},{7,1},{8,10},{9,11},{10,... | collective-permute-start | bytes 2359304 | tf_op jit(solution)/shard_map/ppermute | solution.py:277
  430.3 78.2 %collective-permute-start.48 = (f32[32,6144]{1,0:T(8,128)}, f32[32,6144]{1,0:T(8,128)}, u32[]{:S(2)}, u32[]{:S(2)}) collective-permute-start(f32[32,6144]{1,0:T(8,128)} %get-tuple-element.610), channel_id=1, source_target_pairs={{0,2},{1,3},{2,4},{3,5},{4,6},{5,7},{6,0},{7,1},{8,10},{9,11},{10,... | collective-permute-start | bytes 2359304 | tf_op jit(solution)/shard_map/ppermute | solution.py:277
  431.8 56.4 %collective-permute-start.35 = (f32[32,6144]{1,0:T(8,128)}, f32[32,6144]{1,0:T(8,128)}, u32[]{:S(2)}, u32[]{:S(2)}) collective-permute-start(f32[32,6144]{1,0:T(8,128)} %pad_maximum_fusion.17), channel_id=1, source_target_pairs={{0,6},{1,7},{2,0},{3,1},{4,2},{5,3},{6,4},{7,5},{8,14},{9,15},{10,... | collective-permute-start | bytes 2359304 | tf_op jit(solution)/shard_map/ppermute | solution.py:277
  492.9 40.6 %collective-permute-start.34 = (f32[16,6144]{1,0:T(8,128)}, f32[16,6144]{1,0:T(8,128)S(1)}, u32[]{:S(2)}, u32[]{:S(2)}) collective-permute-start(f32[16,6144]{1,0:T(8,128)} %get-tuple-element.649), channel_id=1, source_target_pairs={{0,2},{1,3},{2,4},{3,5},{4,6},{5,7},{6,0},{7,1},{8,10},{9,11},{10,... | collective-permute-start | bytes 1179656 | tf_op jit(solution)/shard_map/ppermute | solution.py:277
  493.0 48.2 %collective-permute-start.55 = (bf16[64,6144]{1,0:T(8,128)(2,1)}, bf16[64,6144]{1,0:T(8,128)(2,1)}, u32[]{:S(2)}, u32[]{:S(2)}) collective-permute-start(bf16[64,6144]{1,0:T(8,128)(2,1)} %fusion.21.refs_0_), channel_id=1, source_target_pairs={{0,1},{1,0},{2,3},{3,2},{4,5},{5,4},{6,7},{7,6},{8,9},{9,8},{10,11... | collective-permute-start | bytes 2359304 | tf_op jit(solution)/shard_map/ppermute | solution.py:277
  595.5 66.0 %collective-permute-start.60 = (bf16[256,6144]{1,0:T(8,128)(2,1)}, bf16[256,6144]{1,0:T(8,128)(2,1)S(1)}, u32[]{:S(2)}, u32[]{:S(2)}) collective-permute-start(bf16[256,6144]{1,0:T(8,128)(2,1)} %get-tuple-element.428), channel_id=1, source_target_pairs={{0,1},{1,0},{2,3},{3,2},{4,5},{5,4},{6,7},{7,6},{8,9},{9,8},{10,11... | collective-permute-start | bytes 9437192 | tf_op jit(solution)/shard_map/ppermute | solution.py:277
  595.9 36.9 %collective-permute-start.65 = (f32[64,6144]{1,0:T(8,128)S(1)}, f32[64,6144]{1,0:T(8,128)S(1)}, u32[]{:S(2)}, u32[]{:S(2)}) collective-permute-start(f32[64,6144]{1,0:T(8,128)S(1)} %pad_maximum_fusion.7), channel_id=1, source_target_pairs={{0,6},{1,7},{2,0},{3,1},{4,2},{5,3},{6,4},{7,5},{8,14},{9,15},{10,... | collective-permute-start | bytes 4718600 | tf_op jit(solution)/shard_map/ppermute | solution.py:277
  599.2 37.0 %collective-permute-start.66 = (f32[64,6144]{1,0:T(8,128)}, f32[64,6144]{1,0:T(8,128)S(1)}, u32[]{:S(2)}, u32[]{:S(2)}) collective-permute-start(f32[64,6144]{1,0:T(8,128)} %pad_maximum_fusion.6), channel_id=1, source_target_pairs={{0,2},{1,3},{2,4},{3,5},{4,6},{5,7},{6,0},{7,1},{8,10},{9,11},{10,... | collective-permute-start | bytes 4718600 | tf_op jit(solution)/shard_map/ppermute | solution.py:277
  599.2 50.6 %collective-permute-start.63 = (bf16[64,6144]{1,0:T(8,128)(2,1)}, bf16[64,6144]{1,0:T(8,128)(2,1)S(1)}, u32[]{:S(2)}, u32[]{:S(2)}) collective-permute-start(bf16[64,6144]{1,0:T(8,128)(2,1)} %fusion.25.refs_0_), channel_id=1, source_target_pairs={{0,6},{1,7},{2,0},{3,1},{4,2},{5,3},{6,4},{7,5},{8,14},{9,15},{10,... | collective-permute-start | bytes 2359304 | tf_op jit(solution)/shard_map/ppermute | solution.py:277
  601.9 51.2 %collective-permute-start.64 = (bf16[64,6144]{1,0:T(8,128)(2,1)}, bf16[64,6144]{1,0:T(8,128)(2,1)S(1)}, u32[]{:S(2)}, u32[]{:S(2)}) collective-permute-start(bf16[64,6144]{1,0:T(8,128)(2,1)} %fusion.25.refs_0_), channel_id=1, source_target_pairs={{0,2},{1,3},{2,4},{3,5},{4,6},{5,7},{6,0},{7,1},{8,10},{9,11},{10,... | collective-permute-start | bytes 2359304 | tf_op jit(solution)/shard_map/ppermute | solution.py:277
  658.2 38.3 %collective-permute-start.82 = (f32[32,6144]{1,0:T(8,128)S(1)}, f32[32,6144]{1,0:T(8,128)S(1)}, u32[]{:S(2)}, u32[]{:S(2)}) collective-permute-start(f32[32,6144]{1,0:T(8,128)S(1)} %get-tuple-element.602), channel_id=1, source_target_pairs={{0,2},{1,3},{2,4},{3,5},{4,6},{5,7},{6,0},{7,1},{8,10},{9,11},{10,... | collective-permute-start | bytes 2359304 | tf_op jit(solution)/shard_map/ppermute | solution.py:277
  661.5 34.9 %collective-permute-start.81 = (f32[32,6144]{1,0:T(8,128)S(1)}, f32[32,6144]{1,0:T(8,128)S(1)}, u32[]{:S(2)}, u32[]{:S(2)}) collective-permute-start(f32[32,6144]{1,0:T(8,128)S(1)} %get-tuple-element.601), channel_id=1, source_target_pairs={{0,6},{1,7},{2,0},{3,1},{4,2},{5,3},{6,4},{7,5},{8,14},{9,15},{10,... | collective-permute-start | bytes 2359304 | tf_op jit(solution)/shard_map/ppermute | solution.py:277
  700.7 77.1 %collective-permute-start.94 = (f32[64,6144]{1,0:T(8,128)}, f32[64,6144]{1,0:T(8,128)}, u32[]{:S(2)}, u32[]{:S(2)}) collective-permute-start(f32[64,6144]{1,0:T(8,128)} %pad_maximum_fusion.8), channel_id=1, source_target_pairs={{0,2},{1,3},{2,4},{3,5},{4,6},{5,7},{6,0},{7,1},{8,10},{9,11},{10,... | collective-permute-start | bytes 4718600 | tf_op jit(solution)/shard_map/ppermute | solution.py:277
  700.7 73.6 %collective-permute-start.93 = (f32[64,6144]{1,0:T(8,128)}, f32[64,6144]{1,0:T(8,128)}, u32[]{:S(2)}, u32[]{:S(2)}) collective-permute-start(f32[64,6144]{1,0:T(8,128)} %pad_maximum_fusion.9), channel_id=1, source_target_pairs={{0,6},{1,7},{2,0},{3,1},{4,2},{5,3},{6,4},{7,5},{8,14},{9,15},{10,... | collective-permute-start | bytes 4718600 | tf_op jit(solution)/shard_map/ppermute | solution.py:277
  758.3 46.9 %collective-permute-start.83 = (bf16[256,6144]{1,0:T(8,128)(2,1)}, bf16[256,6144]{1,0:T(8,128)(2,1)}, u32[]{:S(2)}, u32[]{:S(2)}) collective-permute-start(bf16[256,6144]{1,0:T(8,128)(2,1)} %get-tuple-element.457), channel_id=1, source_target_pairs={{0,1},{1,0},{2,3},{3,2},{4,5},{5,4},{6,7},{7,6},{8,9},{9,8},{10,11... | collective-permute-start | bytes 9437192 | tf_op jit(solution)/shard_map/ppermute | solution.py:277
  809.8 51.2 %collective-permute-start.106 = (bf16[64,6144]{1,0:T(8,128)(2,1)}, bf16[64,6144]{1,0:T(8,128)(2,1)}, u32[]{:S(2)}, u32[]{:S(2)}) collective-permute-start(bf16[64,6144]{1,0:T(8,128)(2,1)} %fusion.18.refs_0_), channel_id=1, source_target_pairs={{0,1},{1,0},{2,3},{3,2},{4,5},{5,4},{6,7},{7,6},{8,9},{9,8},{10,11... | collective-permute-start | bytes 2359304 | tf_op jit(solution)/shard_map/ppermute | solution.py:277
  810.2 40.1 %collective-permute-start.97 = (f32[32,6144]{1,0:T(8,128)}, f32[32,6144]{1,0:T(8,128)}, u32[]{:S(2)}, u32[]{:S(2)}) collective-permute-start(f32[32,6144]{1,0:T(8,128)} %get-tuple-element.594), channel_id=1, source_target_pairs={{0,2},{1,3},{2,4},{3,5},{4,6},{5,7},{6,0},{7,1},{8,10},{9,11},{10,... | collective-permute-start | bytes 2359304 | tf_op jit(solution)/shard_map/ppermute | solution.py:277
  810.9 50.2 %collective-permute-start.105 = (bf16[32,6144]{1,0:T(8,128)(2,1)}, bf16[32,6144]{1,0:T(8,128)(2,1)S(1)}, u32[]{:S(2)}, u32[]{:S(2)}) collective-permute-start(bf16[32,6144]{1,0:T(8,128)(2,1)} %slice.843), channel_id=1, source_target_pairs={{0,2},{1,3},{2,4},{3,5},{4,6},{5,7},{6,0},{7,1},{8,10},{9,11},{10,... | collective-permute-start | bytes 1179656 | tf_op jit(solution)/shard_map/ppermute | solution.py:277
  811.6 56.7 %collective-permute-start.107 = (bf16[64,6144]{1,0:T(8,128)(2,1)}, bf16[64,6144]{1,0:T(8,128)(2,1)}, u32[]{:S(2)}, u32[]{:S(2)}) collective-permute-start(bf16[64,6144]{1,0:T(8,128)(2,1)} %collective-permute-done.84.refs_1_), channel_id=1, source_target_pairs={{0,1},{1,0},{2,3},{3,2},{4,5},{5,4},{6,7},{7,6},{8,9},{9,8},{10,11... | collective-permute-start | bytes 2359304 | tf_op jit(solution)/shard_map/ppermute | solution.py:277
  811.7 37.4 %collective-permute-start.96 = (f32[32,6144]{1,0:T(8,128)}, f32[32,6144]{1,0:T(8,128)}, u32[]{:S(2)}, u32[]{:S(2)}) collective-permute-start(f32[32,6144]{1,0:T(8,128)} %get-tuple-element.593), channel_id=1, source_target_pairs={{0,6},{1,7},{2,0},{3,1},{4,2},{5,3},{6,4},{7,5},{8,14},{9,15},{10,... | collective-permute-start | bytes 2359304 | tf_op jit(solution)/shard_map/ppermute | solution.py:277
  861.1 37.6 %collective-permute-start.103 = (f32[64,6144]{1,0:T(8,128)}, f32[64,6144]{1,0:T(8,128)}, u32[]{:S(2)}, u32[]{:S(2)}) collective-permute-start(f32[64,6144]{1,0:T(8,128)} %pad_maximum_fusion.10), channel_id=1, source_target_pairs={{0,2},{1,3},{2,4},{3,5},{4,6},{5,7},{6,0},{7,1},{8,10},{9,11},{10,... | collective-permute-start | bytes 4718600 | tf_op jit(solution)/shard_map/ppermute | solution.py:277
  861.1 36.0 %collective-permute-start.102 = (f32[64,6144]{1,0:T(8,128)}, f32[64,6144]{1,0:T(8,128)}, u32[]{:S(2)}, u32[]{:S(2)}) collective-permute-start(f32[64,6144]{1,0:T(8,128)} %pad_maximum_fusion.11), channel_id=1, source_target_pairs={{0,6},{1,7},{2,0},{3,1},{4,2},{5,3},{6,4},{7,5},{8,14},{9,15},{10,... | collective-permute-start | bytes 4718600 | tf_op jit(solution)/shard_map/ppermute | solution.py:277
  867.1 46.9 %collective-permute-start.100 = (bf16[64,6144]{1,0:T(8,128)(2,1)}, bf16[64,6144]{1,0:T(8,128)(2,1)}, u32[]{:S(2)}, u32[]{:S(2)}) collective-permute-start(bf16[64,6144]{1,0:T(8,128)(2,1)} %fusion.22.refs_0_), channel_id=1, source_target_pairs={{0,6},{1,7},{2,0},{3,1},{4,2},{5,3},{6,4},{7,5},{8,14},{9,15},{10,... | collective-permute-start | bytes 2359304 | tf_op jit(solution)/shard_map/ppermute | solution.py:277
  868.3 47.3 %collective-permute-start.101 = (bf16[64,6144]{1,0:T(8,128)(2,1)}, bf16[64,6144]{1,0:T(8,128)(2,1)}, u32[]{:S(2)}, u32[]{:S(2)}) collective-permute-start(bf16[64,6144]{1,0:T(8,128)(2,1)} %fusion.22.refs_0_), channel_id=1, source_target_pairs={{0,2},{1,3},{2,4},{3,5},{4,6},{5,7},{6,0},{7,1},{8,10},{9,11},{10,... | collective-permute-start | bytes 2359304 | tf_op jit(solution)/shard_map/ppermute | solution.py:277
  868.7 92.3 %collective-permute-start.115 = (bf16[64,6144]{1,0:T(8,128)(2,1)}, bf16[64,6144]{1,0:T(8,128)(2,1)}, u32[]{:S(2)}, u32[]{:S(2)}) collective-permute-start(bf16[64,6144]{1,0:T(8,128)(2,1)} %fusion.22.refs_0_), channel_id=1, source_target_pairs={{0,1},{1,0},{2,3},{3,2},{4,5},{5,4},{6,7},{7,6},{8,9},{9,8},{10,11... | collective-permute-start | bytes 2359304 | tf_op jit(solution)/shard_map/ppermute | solution.py:277
  897.1 34.6 %collective-permute-start.99 = (f32[32,6144]{1,0:T(8,128)}, f32[32,6144]{1,0:T(8,128)S(1)}, u32[]{:S(2)}, u32[]{:S(2)}) collective-permute-start(f32[32,6144]{1,0:T(8,128)} %pad_maximum_fusion.19), channel_id=1, source_target_pairs={{0,2},{1,3},{2,4},{3,5},{4,6},{5,7},{6,0},{7,1},{8,10},{9,11},{10,... | collective-permute-start | bytes 2359304 | tf_op jit(solution)/shard_map/ppermute | solution.py:277
  914.0 44.4 %collective-permute-start.121 = (f32[32,6144]{1,0:T(8,128)S(1)}, f32[32,6144]{1,0:T(8,128)S(1)}, u32[]{:S(2)}, u32[]{:S(2)}) collective-permute-start(f32[32,6144]{1,0:T(8,128)S(1)} %get-tuple-element.586), channel_id=1, source_target_pairs={{0,2},{1,3},{2,4},{3,5},{4,6},{5,7},{6,0},{7,1},{8,10},{9,11},{10,... | collective-permute-start | bytes 2359304 | tf_op jit(solution)/shard_map/ppermute | solution.py:277
  916.6 41.7 %collective-permute-start.120 = (f32[32,6144]{1,0:T(8,128)S(1)}, f32[32,6144]{1,0:T(8,128)S(1)}, u32[]{:S(2)}, u32[]{:S(2)}) collective-permute-start(f32[32,6144]{1,0:T(8,128)S(1)} %get-tuple-element.585), channel_id=1, source_target_pairs={{0,6},{1,7},{2,0},{3,1},{4,2},{5,3},{6,4},{7,5},{8,14},{9,15},{10,... | collective-permute-start | bytes 2359304 | tf_op jit(solution)/shard_map/ppermute | solution.py:277
  961.8 36.8 %collective-permute-start.124 = (bf16[64,6144]{1,0:T(8,128)(2,1)S(1)}, bf16[64,6144]{1,0:T(8,128)(2,1)S(1)}, u32[]{:S(2)}, u32[]{:S(2)}) collective-permute-start(bf16[64,6144]{1,0:T(8,128)(2,1)S(1)} %fusion.26.refs_0_), channel_id=1, source_target_pairs={{0,6},{1,7},{2,0},{3,1},{4,2},{5,3},{6,4},{7,5},{8,14},{9,15},{10,... | collective-permute-start | bytes 2359304 | tf_op jit(solution)/shard_map/ppermute | solution.py:277
  965.6 45.9 %collective-permute-start.135 = (bf16[64,6144]{1,0:T(8,128)(2,1)S(1)}, bf16[64,6144]{1,0:T(8,128)(2,1)}, u32[]{:S(2)}, u32[]{:S(2)}) collective-permute-start(bf16[64,6144]{1,0:T(8,128)(2,1)S(1)} %fusion.26.refs_0_), channel_id=1, source_target_pairs={{0,1},{1,0},{2,3},{3,2},{4,5},{5,4},{6,7},{7,6},{8,9},{9,8},{10,11... | collective-permute-start | bytes 2359304 | tf_op jit(solution)/shard_map/ppermute | solution.py:277
  (236 other events, 3172.0 us)

commit v2 on v1

v2 whole, which is shorter than its diff:
```python
import functools

import jax
import jax.numpy as jnp
from jax import lax
from jax.experimental import pallas as pl
from jax.experimental.pallas import tpu as pltpu
from jax.sharding import PartitionSpec as P


EPS = 1e-5
ROPE_BASE = 10000.0
CHUNKS = (2, 2, 2, 1, 1)
CORES = 2
TP_CHIPS = 4

ORDER = (0, 0, 1, 1, 3, 0, 2, 1, 0, 4, 1, 0, 3, 2, 1, 0, 4, 0, 2, 3, 0, 4, 1, 2, 1, 0, 2, 4, 3, 1, 2, 0, 2, 3, 4, 0, 1, 4, 3, 2, 4, 1, 4, 2, 0, 3, 4, 3, 1, 4, 3, 0, 1, 2, 3, 4, 1, 2, 3, 4, 4, 2, 3, 2, 3)
SPLIT = ((0, 0), (0, 1), (1, 0), (1, 1), (2, 0), (2, 1), (3, 1), (4, 1))


def rope_tables(seq_len, head_dim):
    inv_freq = ROPE_BASE ** (-jnp.arange(0, head_dim, 2).astype(jnp.float32) / head_dim)
    angles = jnp.arange(seq_len).astype(jnp.float32)[:, None] * inv_freq[None, :]
    cos_tab = jnp.repeat(jnp.cos(angles), 2, axis=-1)
    sin_half = jnp.sin(angles)
    sin_tab = jnp.stack([-sin_half, sin_half], axis=-1).reshape(seq_len, head_dim)
    return cos_tab, sin_tab


def attend_kernel(first, heads, lens_ref, place_ref, x_ref, gain_ref, cos_ref, sin_ref, wq_ref, wk_ref, wv_ref, wo_ref, k_ref, v_ref, own_ref, other_ref,
                  x_vmem, n_vmem, wq_vmem, wkv_vmem, wo_vmem, q_vmem, kv_vmem, rows_vmem, turned_vmem, part_vmem, x_sem, w_sem, out_sem):
    seq_len, head_dim = cos_ref.shape
    total = x_vmem.shape[0]
    width = x_vmem.shape[1]
    pieces = x_sem.shape[0]
    piece = total // pieces
    x_loads = [pltpu.make_async_copy(x_ref.at[pl.ds(first + i * piece, piece)], x_vmem.at[pl.ds(i * piece, piece)], x_sem.at[i]) for i in range(pieces)]
    w_loads = [
        pltpu.make_async_copy(wq_ref, wq_vmem, w_sem.at[0]),
        pltpu.make_async_copy(wk_ref, wkv_vmem.at[:, pl.ds(0, head_dim)], w_sem.at[1]),
        pltpu.make_async_copy(wv_ref, wkv_vmem.at[:, pl.ds(head_dim, head_dim)], w_sem.at[2]),
        pltpu.make_async_copy(wo_ref, wo_vmem, w_sem.at[3]),
    ]
    for copy in x_loads + w_loads:
        copy.start()
    gain = gain_ref[...].astype(jnp.float32)
    for i in range(pieces):
        x_loads[i].wait()

        @pl.loop(0, piece // 16)
        def _(step):
            here = pl.ds(pl.multiple_of(i * piece + step * 16, 16), 16)
            rows32 = x_vmem[here].astype(jnp.float32)
            inv_rms = lax.rsqrt(jnp.mean(rows32 * rows32, axis=-1, keepdims=True) + EPS)
            n_vmem[here] = (rows32 * inv_rms * gain).astype(jnp.bfloat16)

    w_loads[0].wait()
    for n in range(0, heads * head_dim, 2 * head_dim):
        q_vmem[:, n:n + 2 * head_dim] = jnp.dot(n_vmem[...], wq_vmem[:, n:n + 2 * head_dim], preferred_element_type=jnp.float32)
    w_loads[1].wait()
    w_loads[2].wait()
    kv_vmem[...] = jnp.dot(n_vmem[...], wkv_vmem[...], preferred_element_type=jnp.float32)

    even = lax.broadcasted_iota(jnp.int32, (seq_len, head_dim), 1) % 2 == 0
    row_at = lax.broadcasted_iota(jnp.int32, (seq_len, head_dim), 0)
    query_at = lax.broadcasted_iota(jnp.int32, (seq_len, seq_len), 0)
    key_at = lax.broadcasted_iota(jnp.int32, (seq_len, seq_len), 1)
    cos_tab, sin_tab = cos_ref[...], sin_ref[...]

    def rotary(vecs):
        partner = jnp.where(even, pltpu.roll(vecs, head_dim - 1, 1), pltpu.roll(vecs, 1, 1))
        return vecs * cos_tab + partner * sin_tab

    for seq in range(total // seq_len):
        here = slice(seq * seq_len, (seq + 1) * seq_len)
        length = lens_ref[first // seq_len + seq]
        valid = row_at < length
        keys = jnp.where(valid, rotary(kv_vmem[here, :head_dim]), 0.0).astype(jnp.bfloat16)
        values = jnp.where(valid, kv_vmem[here, head_dim:], 0.0).astype(jnp.bfloat16)
        k_ref[here] = keys
        v_ref[here] = values
        allowed = (key_at <= query_at) & (key_at < length)
        for head in range(heads):
            cols = slice(head * head_dim, (head + 1) * head_dim)
            query = rotary(q_vmem[here, cols]).astype(jnp.bfloat16)
            scores = lax.dot_general(query, keys, (((1,), (1,)), ((), ())), preferred_element_type=jnp.float32) * head_dim ** -0.5
            scores = jnp.where(allowed, scores, -jnp.inf)
            weights = jnp.exp(scores - jnp.max(scores, axis=-1, keepdims=True))
            probs = (weights / jnp.sum(weights, axis=-1, keepdims=True)).astype(jnp.bfloat16)
            rows_vmem[here, cols] = jnp.dot(probs, values, preferred_element_type=jnp.float32)
    block = total // (CORES * TP_CHIPS)
    for c in range(CORES):
        for j in range(TP_CHIPS):
            core = lax.rem(place_ref[1] + c, CORES)
            chip = lax.rem(place_ref[0] + j, TP_CHIPS)
            source = pl.multiple_of((core * TP_CHIPS + chip) * block, block)
            at = (c * TP_CHIPS + j) * block
            turned_vmem[at:at + block] = rows_vmem[pl.ds(source, block)].astype(jnp.bfloat16)
    w_loads[3].wait()
    tiles = out_sem.shape[0] // 2
    step = width // tiles
    half = total // 2
    stores = []
    for tile in range(tiles):
        cols = pl.ds(tile * step, step)
        part_vmem[:, tile * step:(tile + 1) * step] = jnp.dot(turned_vmem[...], wo_vmem[:, tile * step:(tile + 1) * step], preferred_element_type=jnp.float32).astype(jnp.bfloat16)
        stores.append(pltpu.make_async_copy(part_vmem.at[pl.ds(half, half), cols], other_ref.at[:, cols], out_sem.at[2 * tile]))
        stores.append(pltpu.make_async_copy(part_vmem.at[pl.ds(0, half), cols], own_ref.at[:, cols], out_sem.at[2 * tile + 1]))
        if tile:
            stores[-4].start()
            stores[-3].start()
    stores[-2].start()
    stores[-1].start()
    for copy in stores:
        copy.wait()


def attend(first, rows, lens, place, x_flat, gain, cos_tab, sin_tab, w_query, w_key, w_value, w_out):
    seq_len, head_dim = cos_tab.shape
    width, q_width = w_query.shape
    heads = q_width // head_dim
    smem = pl.BlockSpec(memory_space=pltpu.SMEM)
    vmem = pl.BlockSpec(memory_space=pltpu.VMEM)
    hbm = pl.BlockSpec(memory_space=pl.ANY)
    bf16, f32 = jnp.bfloat16, jnp.float32
    return pl.pallas_call(
        functools.partial(attend_kernel, first, heads),
        in_specs=[smem, smem, hbm, vmem, vmem, vmem, hbm, hbm, hbm, hbm],
        out_specs=[vmem, vmem, hbm, hbm],
        out_shape=[jax.ShapeDtypeStruct((rows, head_dim), bf16)] * 2 + [jax.ShapeDtypeStruct((rows // 2, width), bf16)] * 2,
        scratch_shapes=[
            pltpu.VMEM((rows, width), bf16),
            pltpu.VMEM((rows, width), bf16),
            pltpu.VMEM(w_query.shape, bf16),
            pltpu.VMEM((width, 2 * head_dim), bf16),
            pltpu.VMEM(w_out.shape, bf16),
            pltpu.VMEM((rows, q_width), f32),
            pltpu.VMEM((rows, 2 * head_dim), f32),
            pltpu.VMEM((rows, q_width), f32),
            pltpu.VMEM((rows, q_width), bf16),
            pltpu.VMEM((rows, width), bf16),
            pltpu.SemaphoreType.DMA((4,)),
            pltpu.SemaphoreType.DMA((4,)),
            pltpu.SemaphoreType.DMA((2 * max(1, width // 512),)),
        ],
        compiler_params=pltpu.CompilerParams(vmem_limit_bytes=60 * 2**20),
        cost_estimate=pl.CostEstimate(flops=4 * rows * seq_len * q_width + 4 * rows * q_width * width, bytes_accessed=6 * q_width * width + 4 * rows * width, transcendentals=rows * seq_len * heads),
    )(lens, place, x_flat, gain, cos_tab, sin_tab, w_query, w_key, w_value, w_out)


def norm_kernel(rows_ref, gain_ref, out_ref):
    gain = gain_ref[...].astype(jnp.float32)
    for at in range(0, rows_ref.shape[0], 16):
        rows32 = rows_ref[at:at + 16].astype(jnp.float32)
        inv_rms = lax.rsqrt(jnp.mean(rows32 * rows32, axis=-1, keepdims=True) + EPS)
        out_ref[at:at + 16] = (rows32 * inv_rms * gain).astype(jnp.bfloat16)


def norm(rows, gain):
    vmem = pl.BlockSpec(memory_space=pltpu.VMEM)
    return pl.pallas_call(
        norm_kernel,
        in_specs=[vmem, vmem],
        out_specs=vmem,
        out_shape=jax.ShapeDtypeStruct(rows.shape, jnp.bfloat16),
        compiler_params=pltpu.CompilerParams(vmem_limit_bytes=8 * 2**20),
        cost_estimate=pl.CostEstimate(flops=rows.size * 1000, bytes_accessed=4 * rows.size, transcendentals=0),
    )(rows, gain)


def mlp_kernel(count, *refs):
    blocks, (gate_ref, up_ref, down_ref, own_ref, other_ref, rows_ref, total_ref, sem) = refs[:count], refs[count:]
    tile = pl.program_id(0)

    @pl.when(tile == 0)
    def _():
        copies, at = [], 0
        for i, ref in enumerate(blocks):
            copies.append(pltpu.make_async_copy(ref, rows_ref.at[pl.ds(at, ref.shape[0])], sem.at[i]))
            at += ref.shape[0]
        for copy in copies:
            copy.start()
        for copy in copies:
            copy.wait()

    rows = rows_ref[...]
    gate = jnp.dot(rows, gate_ref[...], preferred_element_type=jnp.float32)
    up = jnp.dot(rows, up_ref[...], preferred_element_type=jnp.float32)
    gated = (gate * jax.nn.sigmoid(gate) * up).astype(jnp.bfloat16)
    width = down_ref.shape[1]
    half = rows_ref.shape[0] // 2
    step = min(width, 512)
    last = pl.num_programs(0) - 1

    def column(n, handle):
        cols = slice(n, n + step)
        handle(cols, jnp.dot(gated, down_ref[:, cols], preferred_element_type=jnp.float32))

    @pl.when(tile == 0)
    def _():
        for n in range(0, width, step):
            def first(cols, part):
                total_ref[:, cols] = part

            column(n, first)

    @pl.when((tile > 0) & (tile < last))
    def _():
        for n in range(0, width, step):
            def middle(cols, part):
                total_ref[:, cols] += part

            column(n, middle)

    @pl.when(tile == last)
    def _():
        for n in range(0, width, step):
            def final(cols, part):
                done = (total_ref[:, cols] + part).astype(jnp.bfloat16)
                own_ref[:, cols] = done[:half]
                other_ref[:, cols] = done[half:]

            column(n, final)


def mlp(blocks, w_gate, w_up, w_down, tile=256):
    width, hidden = w_gate.shape
    rows = sum(block.shape[0] for block in blocks)
    half = pl.BlockSpec((rows // 2, width), lambda i: (0, 0))
    return pl.pallas_call(
        functools.partial(mlp_kernel, len(blocks)),
        grid=(hidden // tile,),
        in_specs=[pl.BlockSpec(memory_space=pl.ANY)] * len(blocks) + [pl.BlockSpec((width, tile), lambda i: (0, i))] * 2 + [pl.BlockSpec((tile, width), lambda i: (i, 0))],
        out_specs=[half, half],
        out_shape=[jax.ShapeDtypeStruct((rows // 2, width), jnp.bfloat16)] * 2,
        scratch_shapes=[
            pltpu.VMEM((rows, width), jnp.bfloat16),
            pltpu.VMEM((rows, width), jnp.float32),
            pltpu.SemaphoreType.DMA((len(blocks),)),
        ],
        compiler_params=pltpu.CompilerParams(dimension_semantics=("arbitrary",), vmem_limit_bytes=60 * 2**20),
        cost_estimate=pl.CostEstimate(flops=6 * rows * width * hidden, bytes_accessed=6 * width * hidden + 4 * rows * width, transcendentals=rows * hidden),
    )(*blocks, w_gate, w_up, w_down)


def place_kernel(count, offsets_ref, *refs):
    blocks, (out_ref, buffer, sems) = refs[:count], refs[-3:]
    loads, stores, at = [], [], 0
    for i, ref in enumerate(blocks):
        size = ref.shape[0]
        here = buffer.at[pl.ds(at, size)]
        there = out_ref.at[pl.ds(pl.multiple_of(offsets_ref[i], 16), size)]
        loads.append(pltpu.make_async_copy(ref, here, sems.at[i]))
        stores.append(pltpu.make_async_copy(here, there, sems.at[count + i]))
        at += size
    for copy in loads:
        copy.start()
    for load, store in zip(loads, stores):
        load.wait()
        store.start()
    for copy in stores:
        copy.wait()


def place_blocks(offsets, blocks, result, total):
    count = len(blocks)
    rows, width = sum(block.shape[0] for block in blocks), blocks[0].shape[1]
    hbm = pl.BlockSpec(memory_space=pl.ANY)
    held = () if result is None else (result,)
    return pl.pallas_call(
        functools.partial(place_kernel, count),
        in_specs=[pl.BlockSpec(memory_space=pltpu.SMEM)] + [hbm] * (count + len(held)),
        out_specs=hbm,
        out_shape=jax.ShapeDtypeStruct((total, width), jnp.bfloat16),
        scratch_shapes=[pltpu.VMEM((rows, width), jnp.bfloat16), pltpu.SemaphoreType.DMA((2 * count,))],
        input_output_aliases={count + 1: 0} if held else {},
        cost_estimate=pl.CostEstimate(flops=2 * rows * width * 1024, bytes_accessed=4 * rows * width, transcendentals=0),
    )(offsets, *blocks, *held)


def solution(mesh):
    tp_size = mesh.shape["tp"]
    chips = tp_size // CORES
    to_left = [(i, (i - CORES) % tp_size) for i in range(tp_size)]
    to_right = [(i, (i + CORES) % tp_size) for i in range(tp_size)]
    to_sibling = [(i, i ^ 1) for i in range(tp_size)]

    def send(array, perm):
        return lax.ppermute(array, "tp", perm)

    def layer_body(x, seq_lens, w_query, w_key, w_value, w_out, w_gate, w_up, w_down, attn_gain, mlp_gain, k_cache, v_cache):
        batch_size, seq_len, model_width = x.shape
        head_dim = k_cache.shape[3]
        tp_index = lax.axis_index("tp")
        chip, core = tp_index // CORES, tp_index % CORES
        cos_tab, sin_tab = rope_tables(seq_len, head_dim)
        x_flat = x.reshape(batch_size * seq_len, model_width)
        place = jnp.stack([chip, core]).astype(jnp.int32)
        state = {"last": place, "y": None}
        keys_all, values_all = [None] * len(CHUNKS), [None] * len(CHUNKS)

        def after(*arrays):
            return lax.optimization_barrier((*arrays, state["last"]))[:-1]

        def exchange(own, other, resid, flip, split):
            block = own.shape[0] // chips
            half = block // 2
            got = send(other, to_sibling)
            yield
            own, got = after(own, got)

            def pair(j, begin=0, end=block):
                rows = slice(j * block + begin, j * block + end)
                return own[rows].astype(jnp.float32) + got[rows].astype(jnp.float32)

            if split:
                go_left = jnp.concatenate([pair(2, 0, half), pair(3, half)], axis=0)
                go_right = jnp.concatenate([pair(2, half), pair(1, 0, half)], axis=0)
                state["last"] = go_right
                from_right, from_left = send(go_left, to_left), send(go_right, to_right)
                yield
                own, got, from_right, from_left = after(own, got, from_right, from_left)
                go_left = pair(3, 0, half) + from_right[:half]
                go_right = pair(1, half) + from_left[:half]
                state["last"] = go_right
                far_right, far_left = send(go_left, to_left), send(go_right, to_right)
                yield
                own, got, from_right, from_left, far_right, far_left = after(own, got, from_right, from_left, far_right, far_left)
                total = jnp.concatenate([pair(0, 0, half) + from_left[half:] + far_right, pair(0, half) + from_right[half:] + far_left], axis=0)
            else:
                ahead, back = (1, 3) if flip else (3, 1)
                forward, backward = (to_right, to_left) if flip else (to_left, to_right)
                far, near = pair(2), pair(back)
                state["last"] = near
                far, near = send(far, forward), send(near, backward)
                yield
                own, got, far = after(own, got, far)
                passed = pair(ahead) + far
                state["last"] = passed
                passed = send(passed, forward)
                yield
                own, got, near, passed = after(own, got, near, passed)
                total = pair(0) + near + passed
            return (resid.astype(jnp.float32) + total).astype(jnp.bfloat16)

        def gather(block, flip, split):
            half = block.shape[0] // 2
            state["last"] = block
            right, left = send(block, to_left), send(block, to_right)
            other = [send(block, to_sibling)]
            yield
            if split:
                right, left = after(right, left)
                go_left, go_right = right[:half], left[half:]
                state["last"] = go_right
                opposite = [send(go_left, to_left), send(go_right, to_right)]
            elif flip:
                (left,) = after(left)
                opposite = [send(left, to_right)]
            else:
                (right,) = after(right)
                opposite = [send(right, to_left)]
            right_other, left_other = send(right, to_sibling), send(left, to_sibling)
            yield
            other += [right_other] + [send(part, to_sibling) for part in opposite] + [left_other]
            return [block, right, *opposite, left], other

        def chunk_stages(index):
            first, count = sum(CHUNKS[:index]) * seq_len, CHUNKS[index]
            rows = count * seq_len
            block = rows // tp_size
            (lens,) = after(seq_lens)
            keys, values, own, other = attend(first, rows, lens, place, x_flat, attn_gain[None], cos_tab, sin_tab, w_query, w_key, w_value, w_out)
            keys_all[index], values_all[index] = keys, values
            state["last"] = other
            resid = lax.dynamic_slice(x_flat, (first + core * (rows // CORES) + chip * block, 0), (block, model_width))
            flip, split = index % 2 == 1, (index, 0) in SPLIT
            hidden = yield from exchange(own, other, resid, flip, split)
            own, other = yield from gather(norm(hidden, mlp_gain[None]), not flip, split)
            yield
            blocks = after(*own, *other)
            own, other = mlp(blocks, w_gate, w_up, w_down)
            state["last"] = other
            split = (index, 1) in SPLIT
            out = yield from exchange(own, other, hidden, not flip, split)
            own, other = yield from gather(out, flip, split)
            yield
            blocks = after(*own, *other)
            offsets = []
            for parity in (core, 1 - core):
                for j, shift in ((0, 0), (1, 0), (2, 0)) + (((2, block // 2),) if split else ()) + ((3, 0),):
                    offsets.append(first + parity * (rows // CORES) + (chip + j) % chips * block + shift)
            state["y"] = state["last"] = place_blocks(jnp.stack(offsets), blocks, state["y"], x_flat.shape[0])

        runs = [chunk_stages(index) for index in range(len(CHUNKS))]
        for index in ORDER:
            next(runs[index], None)
        y = state["y"].reshape(x.shape)
        keys = jnp.concatenate(keys_all, axis=0).reshape(batch_size, seq_len, 1, head_dim)
        values = jnp.concatenate(values_all, axis=0).reshape(batch_size, seq_len, 1, head_dim)
        k_cache_out = lax.dynamic_update_slice(k_cache, keys, (0, 0, 0, 0))
        v_cache_out = lax.dynamic_update_slice(v_cache, values, (0, 0, 0, 0))
        return y, k_cache_out, v_cache_out

    cache_spec = P("dp", None, "tp", None)
    return jax.shard_map(layer_body, mesh=mesh, in_specs=(P("dp", None, None), P("dp"), P(None, "tp"), P(None, "tp"), P(None, "tp"), P("tp", None), P(None, "tp"), P(None, "tp"), P("tp", None), P(), P(), cache_spec, cache_spec), out_specs=(P("dp", None, None), cache_spec, cache_spec), check_vma=False)
```

time: 1050 us -> 974 us (0.928)
  Pallas kernels: 308 us -> 381 us
  matrix products: 66.8 us -> 0 us
  waiting for transfers between devices: 337 us -> 300 us
  other arithmetic: 118 us -> 83.3 us
  local copies, waits for them, and re-layouts: 51.3 us -> 37.9 us
    pallas_call x5 -> x10, Pallas kernels: 51.8 us -> 124 us  [the longest x5 123 us: attend(): pl.pallas_call(functools.partial(attend_kernel, first, heads), in_specs=[...]
    dot_general x10 -> x0, matrix products: 66.8 us -> none  [dot(): return jnp.dot(rows, weight, preferred_element_type=jnp.float32)]
    ppermute x140 -> x134, waiting for transfers between devices: 337 us -> 300 us  [send(): return lax.ppermute(array, 'tp', perm)]
    reduce_sum x10 -> x0, other arithmetic: 24.6 us -> none  [rms_norm(): inv_rms = lax.rsqrt(jnp.mean(rows32 * rows32, axis=-1, keepdims=True) + EPS)]
    concatenate x20 -> x16, other arithmetic: 22.9 us -> 15.1 us  [the longest x8 8.5 us: exchange(): go_right = jnp.concatenate([pair(2, half), pair(1, 0, half)], axis=0)]
    unnamed x296 -> x260, local copies, waits for them, and re-layouts: 25.6 us -> 19.2 us
    add x20 -> x18, other arithmetic: 42.4 us -> 40.8 us  [the longest x8 16.8 us: exchange(): pair(0, 0, half) + from_left[half:] + far_right]
    ppermute x140 -> x134, starting transfers between devices: 158 us -> 159 us  [send(): return lax.ppermute(array, 'tp', perm)]
  transfers between devices with their start and end apart: 140 -> 134, of which waited for: 32 -> 32; matrix products, arithmetic and copies ran while one was open for 17% -> 10% of each run, Pallas kernels for 19% -> 33%
where the time goes in v2:
time: 974 us; the launch traced here: 963 us
  Pallas kernels  381 us (39%)
  waiting for transfers between devices  300 us (31%)
  starting transfers between devices  159 us (16%)
  other arithmetic  83.3 us (9%)
  local copies, waits for them, and re-layouts  37.9 us (4%)
    ppermute x134, waiting for transfers between devices, send(): return lax.ppermute(array, 'tp', perm)  300 us
    pallas_call x5, Pallas kernels, mlp(): pl.pallas_call(functools.partial(mlp_kernel, len(blocks)), grid=(hidden /...  230 us
    ppermute x134, starting transfers between devices, send(): return lax.ppermute(array, 'tp', perm)  159 us
    pallas_call x5, Pallas kernels, attend(): pl.pallas_call(functools.partial(attend_kernel, first, heads), in_specs=[...  123 us
    pallas_call x5, Pallas kernels, place_blocks(): pl.pallas_call(functools.partial(place_kernel, count), in_specs=[pl.Block...  26.1 us
  transfers between devices with their start and end apart: 134, of which 32 were waited for; matrix products, arithmetic and copies ran while one was open for 10% of the time, Pallas kernels for 33%

profile of v2, /device:TPU:81, one launch (start us, length us, event | category | flops | bytes accessed | tf_op | source)
XLA Modules:
  0.0 963.1 jit_solution(17029452376692735)
XLA Ops:
  6.5 28.7 %shard_map.148 = (bf16[512,128]{1,0:T(8,128)(2,1)}, bf16[512,128]{1,0:T(8,128)(2,1)}, bf16[256,6144]{1,0:T(8,128)(2,1)}, bf16[256,6144]{1,0:T(8,128)(2,1)}) custom-call(s32[8]{0:T(128)} %lens_ref.4, s32[2]{0:T(128)} %pad_add_fusion.place_ref, bf16[2048,6144]{1,0:T(8,128)(2,1)} %bitcast.64, bf16[1,6144]{1,0:T(2,128)(2,1)} %broadcast_in_dim.27.gain_ref, ...), custom_call_target="tpu_custom_call" | custom-call | flops 10066329600 | bytes 40894464 | tf_op jit(solution)/shard_map/pallas_call | solution.py:126
  37.3 5.5 collective-permute-done
  46.9 28.7 %shard_map.149 = (bf16[512,128]{1,0:T(8,128)(2,1)}, bf16[512,128]{1,0:T(8,128)(2,1)}, bf16[256,6144]{1,0:T(8,128)(2,1)}, bf16[256,6144]{1,0:T(8,128)(2,1)}) custom-call(s32[8]{0:T(128)} %lens_ref.4, s32[2]{0:T(128)} %pad_add_fusion.place_ref, bf16[2048,6144]{1,0:T(8,128)(2,1)} %bitcast.65, bf16[1,6144]{1,0:T(2,128)(2,1)} %broadcast_in_dim.27.gain_ref, ...), custom_call_target="tpu_custom_call" | custom-call | flops 10066329600 | bytes 40894464 | tf_op jit(solution)/shard_map/pallas_call | solution.py:126
  85.4 18.0 %shard_map.150 = (bf16[256,128]{1,0:T(8,128)(2,1)}, bf16[256,128]{1,0:T(8,128)(2,1)}, bf16[128,6144]{1,0:T(8,128)(2,1)}, bf16[128,6144]{1,0:T(8,128)(2,1)}) custom-call(s32[8]{0:T(128)} %lens_ref.4, s32[2]{0:T(128)} %pad_add_fusion.place_ref, bf16[2048,6144]{1,0:T(8,128)(2,1)} %bitcast.66, bf16[1,6144]{1,0:T(2,128)(2,1)} %broadcast_in_dim.27.gain_ref, ...), custom_call_target="tpu_custom_call" | custom-call | flops 5033164800 | bytes 34603008 | tf_op jit(solution)/shard_map/pallas_call | solution.py:126
  103.4 10.9 %collective-permute-done.3 = f32[64,6144]{1,0:T(8,128)} collective-permute-done((f32[64,6144]{1,0:T(8,128)}, f32[64,6144]{1,0:T(8,128)}, u32[]{:S(2)}, u32[]{:S(2)}) %collective-permute-start.3) | collective-permute-done | bytes 1572896 | tf_op jit(solution)/shard_map/ppermute | solution.py:289
  126.4 28.8 %shard_map.151 = (bf16[512,128]{1,0:T(8,128)(2,1)}, bf16[512,128]{1,0:T(8,128)(2,1)}, bf16[256,6144]{1,0:T(8,128)(2,1)}, bf16[256,6144]{1,0:T(8,128)(2,1)}) custom-call(s32[8]{0:T(128)} %lens_ref.4, s32[2]{0:T(128)} %pad_add_fusion.place_ref, bf16[2048,6144]{1,0:T(8,128)(2,1)} %bitcast.67, bf16[1,6144]{1,0:T(2,128)(2,1)} %broadcast_in_dim.27.gain_ref, ...), custom_call_target="tpu_custom_call" | custom-call | flops 10066329600 | bytes 40894464 | tf_op jit(solution)/shard_map/pallas_call | solution.py:126
  155.6 3.5 slice_add_fusion.8
  159.1 9.2 collective-permute-done.5
  168.3 3.8 collective-permute-start.11
  176.6 18.4 %shard_map.153 = (bf16[256,128]{1,0:T(8,128)(2,1)}, bf16[256,128]{1,0:T(8,128)(2,1)}, bf16[128,6144]{1,0:T(8,128)(2,1)}, bf16[128,6144]{1,0:T(8,128)(2,1)}) custom-call(s32[8]{0:T(128)} %lens_ref.4, s32[2]{0:T(128)} %pad_add_fusion.place_ref, bf16[2048,6144]{1,0:T(8,128)(2,1)} %bitcast.69, bf16[1,6144]{1,0:T(2,128)(2,1)} %broadcast_in_dim.27.gain_ref, ...), custom_call_target="tpu_custom_call" | custom-call | flops 5033164800 | bytes 34603008 | tf_op jit(solution)/shard_map/pallas_call | solution.py:126
  204.6 7.1 collective-permute-done.9.refs_1_
  223.3 5.3 collective-permute-done.25.refs_1_
  228.6 6.5 collective-permute-start.19
  248.6 53.4 %shard_map.155 = (bf16[256,6144]{1,0:T(8,128)(2,1)}, bf16[256,6144]{1,0:T(8,128)(2,1)}) custom-call(bf16[64,6144]{1,0:T(8,128)(2,1)} %copy-done.8, bf16[64,6144]{1,0:T(8,128)(2,1)} %copy-done.95, bf16[32,6144]{1,0:T(8,128)(2,1)} %copy-done.118, bf16[32,6144]{1,0:T(8,128)(2,1)} %copy-done.117, bf16[64,6144]{1,0:T(8,128)(2,1)} %collective-permute-done.10.refs_4_, ...), custom_call_target="tpu_custom_call" | custom-call | flops 38654705664 | bytes 88080384 | tf_op jit(solution)/shard_map/pallas_call | solution.py:230
  309.1 13.8 %collective-permute-done.13 = f32[32,6144]{1,0:T(8,128)S(1)} collective-permute-done((f32[32,6144]{1,0:T(8,128)S(1)}, f32[32,6144]{1,0:T(8,128)S(1)}, u32[]{:S(2)}, u32[]{:S(2)}) %collective-permute-start.13) | collective-permute-done | bytes 786464 | tf_op jit(solution)/shard_map/ppermute | solution.py:289
  336.4 12.7 %collective-permute-done.33 = f32[32,6144]{1,0:T(8,128)S(1)} collective-permute-done((f32[32,6144]{1,0:T(8,128)S(1)}, f32[32,6144]{1,0:T(8,128)S(1)}, u32[]{:S(2)}, u32[]{:S(2)}) %collective-permute-start.33) | collective-permute-done | bytes 786464 | tf_op jit(solution)/shard_map/ppermute | solution.py:289
  362.8 53.4 %shard_map.157 = (bf16[256,6144]{1,0:T(8,128)(2,1)}, bf16[256,6144]{1,0:T(8,128)(2,1)}) custom-call(bf16[64,6144]{1,0:T(8,128)(2,1)} %copy-done.6, bf16[64,6144]{1,0:T(8,128)(2,1)} %copy-done.91, bf16[32,6144]{1,0:T(8,128)(2,1)} %copy-done.115, bf16[32,6144]{1,0:T(8,128)(2,1)} %copy-done.114, bf16[64,6144]{1,0:T(8,128)(2,1)} %copy-done.93, ...), custom_call_target="tpu_custom_call" | custom-call | flops 38654705664 | bytes 88080384 | tf_op jit(solution)/shard_map/pallas_call | solution.py:230
  421.5 4.7 collective-permute-done.36.refs_4_
  428.6 5.0 collective-permute-done.32
  435.6 14.9 %collective-permute-done.27 = f32[32,6144]{1,0:T(8,128)S(1)} collective-permute-done((f32[32,6144]{1,0:T(8,128)S(1)}, f32[32,6144]{1,0:T(8,128)S(1)}, u32[]{:S(2)}, u32[]{:S(2)}) %collective-permute-start.27) | collective-permute-done | bytes 786464 | tf_op jit(solution)/shard_map/ppermute | solution.py:289
  459.6 15.9 %collective-permute-done.47.refs_2_ = bf16[32,6144]{1,0:T(8,128)(2,1)S(1)} collective-permute-done((bf16[32,6144]{1,0:T(8,128)(2,1)S(1)}, bf16[32,6144]{1,0:T(8,128)(2,1)S(1)}, u32[]{:S(2)}, u32[]{:S(2)}) %collective-permute-start.47) | collective-permute-done | bytes 393248 | tf_op jit(solution)/shard_map/ppermute | solution.py:289
  475.5 3.9 collective-permute-start.50
  486.2 53.4 %shard_map.160 = (bf16[256,6144]{1,0:T(8,128)(2,1)}, bf16[256,6144]{1,0:T(8,128)(2,1)}) custom-call(bf16[64,6144]{1,0:T(8,128)(2,1)} %copy-done.7, bf16[64,6144]{1,0:T(8,128)(2,1)} %collective-permute-done.35.refs_1_, bf16[32,6144]{1,0:T(8,128)(2,1)} %copy-done.119, bf16[32,6144]{1,0:T(8,128)(2,1)} %copy-done.116, ...), custom_call_target="tpu_custom_call" | custom-call | flops 38654705664 | bytes 88080384 | tf_op jit(solution)/shard_map/pallas_call | solution.py:230
  547.7 39.1 %collective-permute-done.46.refs_1_ = bf16[32,6144]{1,0:T(8,128)(2,1)S(1)} collective-permute-done((bf16[32,6144]{1,0:T(8,128)(2,1)S(1)}, bf16[32,6144]{1,0:T(8,128)(2,1)S(1)}, u32[]{:S(2)}, u32[]{:S(2)}) %collective-permute-start.46) | collective-permute-done | bytes 393248 | tf_op jit(solution)/shard_map/ppermute | solution.py:289
  589.0 14.8 %collective-permute-done.66.refs_1_ = bf16[64,6144]{1,0:T(8,128)(2,1)} collective-permute-done((bf16[64,6144]{1,0:T(8,128)(2,1)}, bf16[64,6144]{1,0:T(8,128)(2,1)}, u32[]{:S(2)}, u32[]{:S(2)}) %collective-permute-start.66) | collective-permute-done | bytes 786464 | tf_op jit(solution)/shard_map/ppermute | solution.py:289
  603.8 3.4 collective-permute-start.70
  622.3 12.0 %collective-permute-done.72.refs_2_ = bf16[32,6144]{1,0:T(8,128)(2,1)S(1)} collective-permute-done((bf16[32,6144]{1,0:T(8,128)(2,1)}, bf16[32,6144]{1,0:T(8,128)(2,1)S(1)}, u32[]{:S(2)}, u32[]{:S(2)}) %collective-permute-start.72) | collective-permute-done | bytes 393248 | tf_op jit(solution)/shard_map/ppermute | solution.py:289
  645.5 35.0 %shard_map.161 = (bf16[128,6144]{1,0:T(8,128)(2,1)}, bf16[128,6144]{1,0:T(8,128)(2,1)}) custom-call(bf16[32,6144]{1,0:T(8,128)(2,1)} %copy-done.5, bf16[32,6144]{1,0:T(8,128)(2,1)} %collective-permute-done.70.refs_1_, bf16[32,6144]{1,0:T(8,128)(2,1)} %copy-done.76, bf16[32,6144]{1,0:T(8,128)(2,1)} %copy-done.62, bf16[32,6144]{1,0:T(8,128)(2,1)} %copy-done.72, ...), custom_call_target="tpu_custom_call" | custom-call | flops 19327352832 | bytes 81788928 | tf_op jit(solution)/shard_map/pallas_call | solution.py:230
  690.3 26.5 %collective-permute-done.69 = f32[64,6144]{1,0:T(8,128)S(1)} collective-permute-done((f32[64,6144]{1,0:T(8,128)}, f32[64,6144]{1,0:T(8,128)S(1)}, u32[]{:S(2)}, u32[]{:S(2)}) %collective-permute-start.69) | collective-permute-done | bytes 1572896 | tf_op jit(solution)/shard_map/ppermute | solution.py:289
  718.9 3.7 collective-permute-done.68
  726.1 3.5 collective-permute-start.81
  730.5 35.1 %shard_map.162 = (bf16[128,6144]{1,0:T(8,128)(2,1)}, bf16[128,6144]{1,0:T(8,128)(2,1)}) custom-call(bf16[32,6144]{1,0:T(8,128)(2,1)} %copy-done.4, bf16[32,6144]{1,0:T(8,128)(2,1)} %copy-done.61, bf16[32,6144]{1,0:T(8,128)(2,1)} %collective-permute-done.57.refs_2_, bf16[32,6144]{1,0:T(8,128)(2,1)} %collective-permute-done.58.refs_3_, ...), custom_call_target="tpu_custom_call" | custom-call | flops 19327352832 | bytes 81788928 | tf_op jit(solution)/shard_map/pallas_call | solution.py:230
  775.3 4.8 collective-permute-done.93.refs_2_
  781.5 15.5 %collective-permute-done.87.refs_1_ = bf16[64,6144]{1,0:T(8,128)(2,1)S(1)} collective-permute-done((bf16[64,6144]{1,0:T(8,128)(2,1)S(1)}, bf16[64,6144]{1,0:T(8,128)(2,1)S(1)}, u32[]{:S(2)}, u32[]{:S(2)}) %collective-permute-start.87) | collective-permute-done | bytes 786464 | tf_op jit(solution)/shard_map/ppermute | solution.py:289
  799.5 5.9 collective-permute-done.85
  812.7 12.6 %collective-permute-done.84 = f32[32,6144]{1,0:T(8,128)S(1)} collective-permute-done((f32[32,6144]{1,0:T(8,128)S(1)}, f32[32,6144]{1,0:T(8,128)S(1)}, u32[]{:S(2)}, u32[]{:S(2)}) %collective-permute-start.84) | collective-permute-done | bytes 786464 | tf_op jit(solution)/shard_map/ppermute | solution.py:289
  833.6 6.3 shard_map.163.refs_10_
  839.9 6.4 collective-permute-done.91
  852.2 11.0 %collective-permute-done.104.refs_2_ = bf16[32,6144]{1,0:T(8,128)(2,1)} collective-permute-done((bf16[32,6144]{1,0:T(8,128)(2,1)}, bf16[32,6144]{1,0:T(8,128)(2,1)}, u32[]{:S(2)}, u32[]{:S(2)}) %collective-permute-start.104) | collective-permute-done | bytes 393248 | tf_op jit(solution)/shard_map/ppermute | solution.py:289
  864.7 6.9 collective-permute-done.89
  876.6 6.7 collective-permute-done.105.refs_3_
  894.2 14.2 %collective-permute-done.127.refs_2_ = bf16[16,6144]{1,0:T(8,128)(2,1)S(1)} collective-permute-done((bf16[16,6144]{1,0:T(8,128)(2,1)S(1)}, bf16[16,6144]{1,0:T(8,128)(2,1)S(1)}, u32[]{:S(2)}, u32[]{:S(2)}) %collective-permute-start.127) | collective-permute-done | bytes 196640 | tf_op jit(solution)/shard_map/ppermute | solution.py:289
  917.2 6.5 shard_map.164.refs_10_
  933.6 4.3 collective-permute-done.120.refs_2_
  942.2 3.5 shard_map.165.refs_10_
  945.7 3.4 collective-permute-done.114.refs_3_
  952.1 6.3 shard_map.166.refs_10_
  959.4 3.5 shard_map.167
  (593 shorter events, 264.3 us)
Async XLA Ops:
  76.1 38.1 %collective-permute-start.4 = (f32[64,6144]{1,0:T(8,128)}, f32[64,6144]{1,0:T(8,128)}, u32[]{:S(2)}, u32[]{:S(2)}) collective-permute-start(f32[64,6144]{1,0:T(8,128)} %pad_maximum_fusion), channel_id=1, source_target_pairs={{0,2},{1,3},{2,4},{3,5},{4,6},{5,7},{6,0},{7,1},{8,10},{9,11},{10,... | collective-permute-start | bytes 4718600 | tf_op jit(solution)/shard_map/ppermute | solution.py:289
  78.2 36.0 %collective-permute-start.3 = (f32[64,6144]{1,0:T(8,128)}, f32[64,6144]{1,0:T(8,128)}, u32[]{:S(2)}, u32[]{:S(2)}) collective-permute-start(f32[64,6144]{1,0:T(8,128)} %pad_maximum_fusion.2), channel_id=1, source_target_pairs={{0,6},{1,7},{2,0},{3,1},{4,2},{5,3},{6,4},{7,5},{8,14},{9,15},{10,... | collective-permute-start | bytes 4718600 | tf_op jit(solution)/shard_map/ppermute | solution.py:289
  84.6 71.0 %collective-permute-start.8 = (f32[64,6144]{1,0:T(8,128)}, f32[64,6144]{1,0:T(8,128)S(1)}, u32[]{:S(2)}, u32[]{:S(2)}) collective-permute-start(f32[64,6144]{1,0:T(8,128)} %pad_maximum_fusion.1), channel_id=1, source_target_pairs={{0,2},{1,3},{2,4},{3,5},{4,6},{5,7},{6,0},{7,1},{8,10},{9,11},{10,... | collective-permute-start | bytes 4718600 | tf_op jit(solution)/shard_map/ppermute | solution.py:289
  115.5 39.7 %collective-permute-start.7 = (f32[64,6144]{1,0:T(8,128)}, f32[64,6144]{1,0:T(8,128)S(1)}, u32[]{:S(2)}, u32[]{:S(2)}) collective-permute-start(f32[64,6144]{1,0:T(8,128)} %pad_maximum_fusion.3), channel_id=1, source_target_pairs={{0,6},{1,7},{2,0},{3,1},{4,2},{5,3},{6,4},{7,5},{8,14},{9,15},{10,... | collective-permute-start | bytes 4718600 | tf_op jit(solution)/shard_map/ppermute | solution.py:289
  121.9 46.4 %collective-permute-start.6 = (f32[32,6144]{1,0:T(8,128)}, f32[32,6144]{1,0:T(8,128)}, u32[]{:S(2)}, u32[]{:S(2)}) collective-permute-start(f32[32,6144]{1,0:T(8,128)} %get-tuple-element.571), channel_id=1, source_target_pairs={{0,2},{1,3},{2,4},{3,5},{4,6},{5,7},{6,0},{7,1},{8,10},{9,11},{10,... | collective-permute-start | bytes 2359304 | tf_op jit(solution)/shard_map/ppermute | solution.py:289
  121.9 91.2 %collective-permute-start.2 = (bf16[128,6144]{1,0:T(8,128)(2,1)}, bf16[128,6144]{1,0:T(8,128)(2,1)}, u32[]{:S(2)}, u32[]{:S(2)}) collective-permute-start(bf16[128,6144]{1,0:T(8,128)(2,1)} %get-tuple-element.278), channel_id=1, source_target_pairs={{0,1},{1,0},{2,3},{3,2},{4,5},{5,4},{6,7},{7,6},{8,9},{9,8},{10,11... | collective-permute-start | bytes 4718600 | tf_op jit(solution)/shard_map/ppermute | solution.py:289
  123.4 44.9 %collective-permute-start.5 = (f32[32,6144]{1,0:T(8,128)}, f32[32,6144]{1,0:T(8,128)}, u32[]{:S(2)}, u32[]{:S(2)}) collective-permute-start(f32[32,6144]{1,0:T(8,128)} %get-tuple-element.572), channel_id=1, source_target_pairs={{0,6},{1,7},{2,0},{3,1},{4,2},{5,3},{6,4},{7,5},{8,14},{9,15},{10,... | collective-permute-start | bytes 2359304 | tf_op jit(solution)/shard_map/ppermute | solution.py:289
  155.2 62.0 %collective-permute-start.14 = (bf16[256,6144]{1,0:T(8,128)(2,1)}, bf16[256,6144]{1,0:T(8,128)(2,1)}, u32[]{:S(2)}, u32[]{:S(2)}) collective-permute-start(bf16[256,6144]{1,0:T(8,128)(2,1)} %get-tuple-element.284), channel_id=1, source_target_pairs={{0,1},{1,0},{2,3},{3,2},{4,5},{5,4},{6,7},{7,6},{8,9},{9,8},{10,11... | collective-permute-start | bytes 9437192 | tf_op jit(solution)/shard_map/ppermute | solution.py:289
  159.1 38.3 %collective-permute-start.12 = (f32[32,6144]{1,0:T(8,128)}, f32[32,6144]{1,0:T(8,128)}, u32[]{:S(2)}, u32[]{:S(2)}) collective-permute-start(f32[32,6144]{1,0:T(8,128)} %get-tuple-element.564), channel_id=1, source_target_pairs={{0,2},{1,3},{2,4},{3,5},{4,6},{5,7},{6,0},{7,1},{8,10},{9,11},{10,... | collective-permute-start | bytes 2359304 | tf_op jit(solution)/shard_map/ppermute | solution.py:289
  197.4 44.5 %collective-permute-start.24 = (bf16[128,6144]{1,0:T(8,128)(2,1)}, bf16[128,6144]{1,0:T(8,128)(2,1)S(1)}, u32[]{:S(2)}, u32[]{:S(2)}) collective-permute-start(bf16[128,6144]{1,0:T(8,128)(2,1)} %get-tuple-element.296), channel_id=1, source_target_pairs={{0,1},{1,0},{2,3},{3,2},{4,5},{5,4},{6,7},{7,6},{8,9},{9,8},{10,11... | collective-permute-start | bytes 4718600 | tf_op jit(solution)/shard_map/ppermute | solution.py:289
  243.6 60.4 %collective-permute-start.16 = (f32[64,6144]{1,0:T(8,128)}, f32[64,6144]{1,0:T(8,128)}, u32[]{:S(2)}, u32[]{:S(2)}) collective-permute-start(f32[64,6144]{1,0:T(8,128)} %pad_maximum_fusion.5), channel_id=1, source_target_pairs={{0,2},{1,3},{2,4},{3,5},{4,6},{5,7},{6,0},{7,1},{8,10},{9,11},{10,... | collective-permute-start | bytes 4718600 | tf_op jit(solution)/shard_map/ppermute | solution.py:289
  243.8 60.5 %collective-permute-start.15 = (f32[64,6144]{1,0:T(8,128)}, f32[64,6144]{1,0:T(8,128)}, u32[]{:S(2)}, u32[]{:S(2)}) collective-permute-start(f32[64,6144]{1,0:T(8,128)} %pad_maximum_fusion.4), channel_id=1, source_target_pairs={{0,6},{1,7},{2,0},{3,1},{4,2},{5,3},{6,4},{7,5},{8,14},{9,15},{10,... | collective-permute-start | bytes 4718600 | tf_op jit(solution)/shard_map/ppermute | solution.py:289
  302.8 52.5 %collective-permute-start.41 = (bf16[64,6144]{1,0:T(8,128)(2,1)S(1)}, bf16[64,6144]{1,0:T(8,128)(2,1)S(1)}, u32[]{:S(2)}, u32[]{:S(2)}) collective-permute-start(bf16[64,6144]{1,0:T(8,128)(2,1)S(1)} %shard_map.154.refs_0_), channel_id=1, source_target_pairs={{0,1},{1,0},{2,3},{3,2},{4,5},{5,4},{6,7},{7,6},{8,9},{9,8},{10,11... | collective-permute-start | bytes 2359304 | tf_op jit(solution)/shard_map/ppermute | solution.py:289
  304.0 32.3 %collective-permute-start.40 = (bf16[32,6144]{1,0:T(8,128)(2,1)S(1)}, bf16[32,6144]{1,0:T(8,128)(2,1)S(1)}, u32[]{:S(2)}, u32[]{:S(2)}) collective-permute-start(bf16[32,6144]{1,0:T(8,128)(2,1)S(1)} %slice.630), channel_id=1, source_target_pairs={{0,2},{1,3},{2,4},{3,5},{4,6},{5,7},{6,0},{7,1},{8,10},{9,11},{10,... | collective-permute-start | bytes 1179656 | tf_op jit(solution)/shard_map/ppermute | solution.py:289
  355.4 71.8 %collective-permute-start.31 = (f32[32,6144]{1,0:T(8,128)}, f32[32,6144]{1,0:T(8,128)}, u32[]{:S(2)}, u32[]{:S(2)}) collective-permute-start(f32[32,6144]{1,0:T(8,128)} %get-tuple-element.594), channel_id=1, source_target_pairs={{0,2},{1,3},{2,4},{3,5},{4,6},{5,7},{6,0},{7,1},{8,10},{9,11},{10,... | collective-permute-start | bytes 2359304 | tf_op jit(solution)/shard_map/ppermute | solution.py:289
  355.7 60.6 %collective-permute-start.38 = (f32[64,6144]{1,0:T(8,128)}, f32[64,6144]{1,0:T(8,128)S(1)}, u32[]{:S(2)}, u32[]{:S(2)}) collective-permute-start(f32[64,6144]{1,0:T(8,128)} %pad_maximum_fusion.6), channel_id=1, source_target_pairs={{0,2},{1,3},{2,4},{3,5},{4,6},{5,7},{6,0},{7,1},{8,10},{9,11},{10,... | collective-permute-start | bytes 4718600 | tf_op jit(solution)/shard_map/ppermute | solution.py:289
  357.2 63.1 %collective-permute-start.35 = (bf16[64,6144]{1,0:T(8,128)(2,1)S(1)}, bf16[64,6144]{1,0:T(8,128)(2,1)}, u32[]{:S(2)}, u32[]{:S(2)}) collective-permute-start(bf16[64,6144]{1,0:T(8,128)(2,1)S(1)} %shard_map.156.refs_0_), channel_id=1, source_target_pairs={{0,6},{1,7},{2,0},{3,1},{4,2},{5,3},{6,4},{7,5},{8,14},{9,15},{10,... | collective-permute-start | bytes 2359304 | tf_op jit(solution)/shard_map/ppermute | solution.py:289
  358.4 67.7 %collective-permute-start.36 = (bf16[64,6144]{1,0:T(8,128)(2,1)S(1)}, bf16[64,6144]{1,0:T(8,128)(2,1)}, u32[]{:S(2)}, u32[]{:S(2)}) collective-permute-start(bf16[64,6144]{1,0:T(8,128)(2,1)S(1)} %shard_map.156.refs_0_), channel_id=1, source_target_pairs={{0,2},{1,3},{2,4},{3,5},{4,6},{5,7},{6,0},{7,1},{8,10},{9,11},{10,... | collective-permute-start | bytes 2359304 | tf_op jit(solution)/shard_map/ppermute | solution.py:289
  360.1 56.1 %collective-permute-start.37 = (f32[64,6144]{1,0:T(8,128)}, f32[64,6144]{1,0:T(8,128)}, u32[]{:S(2)}, u32[]{:S(2)}) collective-permute-start(f32[64,6144]{1,0:T(8,128)} %pad_maximum_fusion.7), channel_id=1, source_target_pairs={{0,6},{1,7},{2,0},{3,1},{4,2},{5,3},{6,4},{7,5},{8,14},{9,15},{10,... | collective-permute-start | bytes 4718600 | tf_op jit(solution)/shard_map/ppermute | solution.py:289
  416.3 39.8 %collective-permute-start.56 = (bf16[256,6144]{1,0:T(8,128)(2,1)}, bf16[256,6144]{1,0:T(8,128)(2,1)S(1)}, u32[]{:S(2)}, u32[]{:S(2)}) collective-permute-start(bf16[256,6144]{1,0:T(8,128)(2,1)} %get-tuple-element.355), channel_id=1, source_target_pairs={{0,1},{1,0},{2,3},{3,2},{4,5},{5,4},{6,7},{7,6},{8,9},{9,8},{10,11... | collective-permute-start | bytes 9437192 | tf_op jit(solution)/shard_map/ppermute | solution.py:289
  420.3 30.2 %collective-permute-start.27 = (f32[32,6144]{1,0:T(8,128)S(1)}, f32[32,6144]{1,0:T(8,128)S(1)}, u32[]{:S(2)}, u32[]{:S(2)}) collective-permute-start(f32[32,6144]{1,0:T(8,128)S(1)} %copy-done.53), channel_id=1, source_target_pairs={{0,6},{1,7},{2,0},{3,1},{4,2},{5,3},{6,4},{7,5},{8,14},{9,15},{10,... | collective-permute-start | bytes 2359304 | tf_op jit(solution)/shard_map/ppermute | solution.py:289
  427.2 55.9 %collective-permute-start.49 = (bf16[64,6144]{1,0:T(8,128)(2,1)S(1)}, bf16[64,6144]{1,0:T(8,128)(2,1)S(1)}, u32[]{:S(2)}, u32[]{:S(2)}) collective-permute-start(bf16[64,6144]{1,0:T(8,128)(2,1)S(1)} %shard_map.156.refs_0_), channel_id=1, source_target_pairs={{0,1},{1,0},{2,3},{3,2},{4,5},{5,4},{6,7},{7,6},{8,9},{9,8},{10,11... | collective-permute-start | bytes 2359304 | tf_op jit(solution)/shard_map/ppermute | solution.py:289
  433.6 46.2 %collective-permute-start.55 = (f32[32,6144]{1,0:T(8,128)S(1)}, f32[32,6144]{1,0:T(8,128)S(1)}, u32[]{:S(2)}, u32[]{:S(2)}) collective-permute-start(f32[32,6144]{1,0:T(8,128)S(1)} %get-tuple-element.548), channel_id=1, source_target_pairs={{0,2},{1,3},{2,4},{3,5},{4,6},{5,7},{6,0},{7,1},{8,10},{9,11},{10,... | collective-permute-start | bytes 2359304 | tf_op jit(solution)/shard_map/ppermute | solution.py:289
  483.9 63.3 %collective-permute-start.71 = (bf16[32,6144]{1,0:T(8,128)(2,1)S(1)}, bf16[32,6144]{1,0:T(8,128)(2,1)S(1)}, u32[]{:S(2)}, u32[]{:S(2)}) collective-permute-start(bf16[32,6144]{1,0:T(8,128)(2,1)S(1)} %shard_map.158.refs_0_), channel_id=1, source_target_pairs={{0,2},{1,3},{2,4},{3,5},{4,6},{5,7},{6,0},{7,1},{8,10},{9,11},{10,... | collective-permute-start | bytes 1179656 | tf_op jit(solution)/shard_map/ppermute | solution.py:289
  539.6 97.2 %collective-permute-start.63 = (bf16[256,6144]{1,0:T(8,128)(2,1)}, bf16[256,6144]{1,0:T(8,128)(2,1)}, u32[]{:S(2)}, u32[]{:S(2)}) collective-permute-start(bf16[256,6144]{1,0:T(8,128)(2,1)} %get-tuple-element.389), channel_id=1, source_target_pairs={{0,1},{1,0},{2,3},{3,2},{4,5},{5,4},{6,7},{7,6},{8,9},{9,8},{10,11... | collective-permute-start | bytes 9437192 | tf_op jit(solution)/shard_map/ppermute | solution.py:289
  541.6 74.5 %collective-permute-start.64 = (f32[64,6144]{1,0:T(8,128)}, f32[64,6144]{1,0:T(8,128)}, u32[]{:S(2)}, u32[]{:S(2)}) collective-permute-start(f32[64,6144]{1,0:T(8,128)} %pad_maximum_fusion.9), channel_id=1, source_target_pairs={{0,6},{1,7},{2,0},{3,1},{4,2},{5,3},{6,4},{7,5},{8,14},{9,15},{10,... | collective-permute-start | bytes 4718600 | tf_op jit(solution)/shard_map/ppermute | solution.py:289
  544.5 73.4 %collective-permute-start.65 = (f32[64,6144]{1,0:T(8,128)}, f32[64,6144]{1,0:T(8,128)}, u32[]{:S(2)}, u32[]{:S(2)}) collective-permute-start(f32[64,6144]{1,0:T(8,128)} %pad_maximum_fusion.8), channel_id=1, source_target_pairs={{0,2},{1,3},{2,4},{3,5},{4,6},{5,7},{6,0},{7,1},{8,10},{9,11},{10,... | collective-permute-start | bytes 4718600 | tf_op jit(solution)/shard_map/ppermute | solution.py:289
  544.5 42.3 %collective-permute-start.46 = (bf16[32,6144]{1,0:T(8,128)(2,1)S(1)}, bf16[32,6144]{1,0:T(8,128)(2,1)S(1)}, u32[]{:S(2)}, u32[]{:S(2)}) collective-permute-start(bf16[32,6144]{1,0:T(8,128)(2,1)S(1)} %shard_map.159.refs_0_), channel_id=1, source_target_pairs={{0,6},{1,7},{2,0},{3,1},{4,2},{5,3},{6,4},{7,5},{8,14},{9,15},{10,... | collective-permute-start | bytes 1179656 | tf_op jit(solution)/shard_map/ppermute | solution.py:289
  547.2 56.6 %collective-permute-start.66 = (bf16[64,6144]{1,0:T(8,128)(2,1)}, bf16[64,6144]{1,0:T(8,128)(2,1)}, u32[]{:S(2)}, u32[]{:S(2)}) collective-permute-start(bf16[64,6144]{1,0:T(8,128)(2,1)} %fusion.3.refs_0_), channel_id=1, source_target_pairs={{0,6},{1,7},{2,0},{3,1},{4,2},{5,3},{6,4},{7,5},{8,14},{9,15},{10,... | collective-permute-start | bytes 2359304 | tf_op jit(solution)/shard_map/ppermute | solution.py:289
  639.8 86.3 %collective-permute-start.59 = (bf16[32,6144]{1,0:T(8,128)(2,1)S(1)}, bf16[32,6144]{1,0:T(8,128)(2,1)}, u32[]{:S(2)}, u32[]{:S(2)}) collective-permute-start(bf16[32,6144]{1,0:T(8,128)(2,1)S(1)} %shard_map.159.refs_0_), channel_id=1, source_target_pairs={{0,1},{1,0},{2,3},{3,2},{4,5},{5,4},{6,7},{7,6},{8,9},{9,8},{10,11... | collective-permute-start | bytes 1179656 | tf_op jit(solution)/shard_map/ppermute | solution.py:289
  640.3 89.4 %collective-permute-start.62 = (bf16[32,6144]{1,0:T(8,128)(2,1)}, bf16[32,6144]{1,0:T(8,128)(2,1)}, u32[]{:S(2)}, u32[]{:S(2)}) collective-permute-start(bf16[32,6144]{1,0:T(8,128)(2,1)} %collective-permute-done.58.refs_3_), channel_id=1, source_target_pairs={{0,1},{1,0},{2,3},{3,2},{4,5},{5,4},{6,7},{7,6},{8,9},{9,8},{10,11... | collective-permute-start | bytes 1179656 | tf_op jit(solution)/shard_map/ppermute | solution.py:289
  640.4 49.6 %collective-permute-start.57 = (bf16[32,6144]{1,0:T(8,128)(2,1)S(1)}, bf16[32,6144]{1,0:T(8,128)(2,1)}, u32[]{:S(2)}, u32[]{:S(2)}) collective-permute-start(bf16[32,6144]{1,0:T(8,128)(2,1)S(1)} %collective-permute-done.46.refs_1_), channel_id=1, source_target_pairs={{0,6},{1,7},{2,0},{3,1},{4,2},{5,3},{6,4},{7,5},{8,14},{9,15},{10,... | collective-permute-start | bytes 1179656 | tf_op jit(solution)/shard_map/ppermute | solution.py:289
  641.9 38.9 %collective-permute-start.79 = (f32[32,6144]{1,0:T(8,128)}, f32[32,6144]{1,0:T(8,128)}, u32[]{:S(2)}, u32[]{:S(2)}) collective-permute-start(f32[32,6144]{1,0:T(8,128)} %get-tuple-element.536), channel_id=1, source_target_pairs={{0,2},{1,3},{2,4},{3,5},{4,6},{5,7},{6,0},{7,1},{8,10},{9,11},{10,... | collective-permute-start | bytes 2359304 | tf_op jit(solution)/shard_map/ppermute | solution.py:289
  643.4 37.2 %collective-permute-start.78 = (f32[32,6144]{1,0:T(8,128)}, f32[32,6144]{1,0:T(8,128)}, u32[]{:S(2)}, u32[]{:S(2)}) collective-permute-start(f32[32,6144]{1,0:T(8,128)} %get-tuple-element.535), channel_id=1, source_target_pairs={{0,6},{1,7},{2,0},{3,1},{4,2},{5,3},{6,4},{7,5},{8,14},{9,15},{10,... | collective-permute-start | bytes 2359304 | tf_op jit(solution)/shard_map/ppermute | solution.py:289
  680.6 36.2 %collective-permute-start.69 = (f32[64,6144]{1,0:T(8,128)}, f32[64,6144]{1,0:T(8,128)S(1)}, u32[]{:S(2)}, u32[]{:S(2)}) collective-permute-start(f32[64,6144]{1,0:T(8,128)} %pad_maximum_fusion.11), channel_id=1, source_target_pairs={{0,2},{1,3},{2,4},{3,5},{4,6},{5,7},{6,0},{7,1},{8,10},{9,11},{10,... | collective-permute-start | bytes 4718600 | tf_op jit(solution)/shard_map/ppermute | solution.py:289
  686.0 36.7 %collective-permute-start.68 = (f32[64,6144]{1,0:T(8,128)S(1)}, f32[64,6144]{1,0:T(8,128)S(1)}, u32[]{:S(2)}, u32[]{:S(2)}) collective-permute-start(f32[64,6144]{1,0:T(8,128)S(1)} %pad_maximum_fusion.10), channel_id=1, source_target_pairs={{0,6},{1,7},{2,0},{3,1},{4,2},{5,3},{6,4},{7,5},{8,14},{9,15},{10,... | collective-permute-start | bytes 4718600 | tf_op jit(solution)/shard_map/ppermute | solution.py:289
  690.0 39.6 %collective-permute-start.60 = (bf16[32,6144]{1,0:T(8,128)(2,1)S(1)}, bf16[32,6144]{1,0:T(8,128)(2,1)S(1)}, u32[]{:S(2)}, u32[]{:S(2)}) collective-permute-start(bf16[32,6144]{1,0:T(8,128)(2,1)S(1)} %collective-permute-done.46.refs_1_), channel_id=1, source_target_pairs={{0,1},{1,0},{2,3},{3,2},{4,5},{5,4},{6,7},{7,6},{8,9},{9,8},{10,11... | collective-permute-start | bytes 1179656 | tf_op jit(solution)/shard_map/ppermute | solution.py:289
  722.7 49.5 %collective-permute-start.82 = (f32[32,6144]{1,0:T(8,128)}, f32[32,6144]{1,0:T(8,128)}, u32[]{:S(2)}, u32[]{:S(2)}) collective-permute-start(f32[32,6144]{1,0:T(8,128)} %pad_maximum_fusion.12), channel_id=1, source_target_pairs={{0,2},{1,3},{2,4},{3,5},{4,6},{5,7},{6,0},{7,1},{8,10},{9,11},{10,... | collective-permute-start | bytes 2359304 | tf_op jit(solution)/shard_map/ppermute | solution.py:289
  726.1 44.7 %collective-permute-start.81 = (f32[32,6144]{1,0:T(8,128)S(1)}, f32[32,6144]{1,0:T(8,128)}, u32[]{:S(2)}, u32[]{:S(2)}) collective-permute-start(f32[32,6144]{1,0:T(8,128)S(1)} %pad_maximum_fusion.13), channel_id=1, source_target_pairs={{0,6},{1,7},{2,0},{3,1},{4,2},{5,3},{6,4},{7,5},{8,14},{9,15},{10,... | collective-permute-start | bytes 2359304 | tf_op jit(solution)/shard_map/ppermute | solution.py:289
  773.5 31.9 %collective-permute-start.85 = (f32[16,6144]{1,0:T(8,128)S(1)}, f32[16,6144]{1,0:T(8,128)S(1)}, u32[]{:S(2)}, u32[]{:S(2)}) collective-permute-start(f32[16,6144]{1,0:T(8,128)S(1)} %get-tuple-element.583), channel_id=1, source_target_pairs={{0,6},{1,7},{2,0},{3,1},{4,2},{5,3},{6,4},{7,5},{8,14},{9,15},{10,... | collective-permute-start | bytes 1179656 | tf_op jit(solution)/shard_map/ppermute | solution.py:289
  774.9 30.5 %collective-permute-start.86 = (f32[16,6144]{1,0:T(8,128)S(1)}, f32[16,6144]{1,0:T(8,128)S(1)}, u32[]{:S(2)}, u32[]{:S(2)}) collective-permute-start(f32[16,6144]{1,0:T(8,128)S(1)} %get-tuple-element.584), channel_id=1, source_target_pairs={{0,2},{1,3},{2,4},{3,5},{4,6},{5,7},{6,0},{7,1},{8,10},{9,11},{10,... | collective-permute-start | bytes 1179656 | tf_op jit(solution)/shard_map/ppermute | solution.py:289
  780.1 46.8 %collective-permute-start.95 = (bf16[64,6144]{1,0:T(8,128)(2,1)}, bf16[64,6144]{1,0:T(8,128)(2,1)S(1)}, u32[]{:S(2)}, u32[]{:S(2)}) collective-permute-start(bf16[64,6144]{1,0:T(8,128)(2,1)} %fusion.3.refs_0_), channel_id=1, source_target_pairs={{0,1},{1,0},{2,3},{3,2},{4,5},{5,4},{6,7},{7,6},{8,9},{9,8},{10,11... | collective-permute-start | bytes 2359304 | tf_op jit(solution)/shard_map/ppermute | solution.py:289
  797.3 30.0 %collective-permute-start.97 = (bf16[32,6144]{1,0:T(8,128)(2,1)S(1)}, bf16[32,6144]{1,0:T(8,128)(2,1)S(1)}, u32[]{:S(2)}, u32[]{:S(2)}) collective-permute-start(bf16[32,6144]{1,0:T(8,128)(2,1)S(1)} %collective-permute-done.93.refs_2_), channel_id=1, source_target_pairs={{0,1},{1,0},{2,3},{3,2},{4,5},{5,4},{6,7},{7,6},{8,9},{9,8},{10,11... | collective-permute-start | bytes 1179656 | tf_op jit(solution)/shard_map/ppermute | solution.py:289
  830.7 45.3 %collective-permute-start.106 = (bf16[64,6144]{1,0:T(8,128)(2,1)S(1)}, bf16[64,6144]{1,0:T(8,128)(2,1)}, u32[]{:S(2)}, u32[]{:S(2)}) collective-permute-start(bf16[64,6144]{1,0:T(8,128)(2,1)S(1)} %fusion.4.refs_0_), channel_id=1, source_target_pairs={{0,1},{1,0},{2,3},{3,2},{4,5},{5,4},{6,7},{7,6},{8,9},{9,8},{10,11... | collective-permute-start | bytes 2359304 | tf_op jit(solution)/shard_map/ppermute | solution.py:289
  831.7 44.4 %collective-permute-start.111 = (bf16[32,6144]{1,0:T(8,128)(2,1)}, bf16[32,6144]{1,0:T(8,128)(2,1)}, u32[]{:S(2)}, u32[]{:S(2)}) collective-permute-start(bf16[32,6144]{1,0:T(8,128)(2,1)} %fusion.6.refs_0_), channel_id=1, source_target_pairs={{0,6},{1,7},{2,0},{3,1},{4,2},{5,3},{6,4},{7,5},{8,14},{9,15},{10,... | collective-permute-start | bytes 1179656 | tf_op jit(solution)/shard_map/ppermute | solution.py:289
  832.7 30.5 %collective-permute-start.104 = (bf16[32,6144]{1,0:T(8,128)(2,1)}, bf16[32,6144]{1,0:T(8,128)(2,1)}, u32[]{:S(2)}, u32[]{:S(2)}) collective-permute-start(bf16[32,6144]{1,0:T(8,128)(2,1)} %slice.761), channel_id=1, source_target_pairs={{0,6},{1,7},{2,0},{3,1},{4,2},{5,3},{6,4},{7,5},{8,14},{9,15},{10,... | collective-permute-start | bytes 1179656 | tf_op jit(solution)/shard_map/ppermute | solution.py:289
  885.1 30.4 %collective-permute-start.102 = (bf16[64,6144]{1,0:T(8,128)(2,1)S(1)}, bf16[64,6144]{1,0:T(8,128)(2,1)S(1)}, u32[]{:S(2)}, u32[]{:S(2)}) collective-permute-start(bf16[64,6144]{1,0:T(8,128)(2,1)S(1)} %fusion.5.refs_0_), channel_id=1, source_target_pairs={{0,6},{1,7},{2,0},{3,1},{4,2},{5,3},{6,4},{7,5},{8,14},{9,15},{10,... | collective-permute-start | bytes 2359304 | tf_op jit(solution)/shard_map/ppermute | solution.py:289
  886.6 29.6 %collective-permute-start.103 = (bf16[64,6144]{1,0:T(8,128)(2,1)S(1)}, bf16[64,6144]{1,0:T(8,128)(2,1)S(1)}, u32[]{:S(2)}, u32[]{:S(2)}) collective-permute-start(bf16[64,6144]{1,0:T(8,128)(2,1)S(1)} %fusion.5.refs_0_), channel_id=1, source_target_pairs={{0,2},{1,3},{2,4},{3,5},{4,6},{5,7},{6,0},{7,1},{8,10},{9,11},{10,... | collective-permute-start | bytes 2359304 | tf_op jit(solution)/shard_map/ppermute | solution.py:289
  (212 other events, 3701.6 us)
